TPU v7x, 64 devices: a 2x2x8 block of a 4x4x8 slice. The times are simulated.
64 devices in a mesh: dp: 4 (over x, y), ep: 16 (over z, core).
Axes of the slice: x: 2, y: 2, z: 8, core: 2. Of those that a mesh axis runs over, the one named last changes fastest.
The devices are a block of a 4x4x8 slice.
Arguments:
- tok_in: bfloat16 [2048, 2048], P(('dp', 'ep')), parts along dimension 0
- lat_cache: bfloat16 [2048, 64, 512], P(('dp', 'ep')), parts along dimension 0
- rope_cache: bfloat16 [2048, 64, 64], P(('dp', 'ep')), parts along dimension 0
- tok_pos: int32 [2048], P(('dp', 'ep')), parts along dimension 0
- expert_ids: int32 [2048, 6], P(('dp', 'ep')), parts along dimension 0
- attn_gain: bfloat16 [2048], replicated
- w_query: bfloat16 [2048, 3072], replicated
- w_kvdown: bfloat16 [2048, 576], replicated
- w_ukey: bfloat16 [16, 128, 512], replicated
- w_uval: bfloat16 [16, 512, 128], replicated
- w_out: bfloat16 [2048, 2048], replicated
- ffn_gain: bfloat16 [2048], replicated
- w_router: bfloat16 [2048, 64], replicated
- sh_gate: bfloat16 [2048, 2816], replicated
- sh_up: bfloat16 [2048, 2816], replicated
- sh_down: bfloat16 [2816, 2048], replicated
- ex_gate: bfloat16 [64, 2048, 1408], P('ep')
- ex_up: bfloat16 [64, 2048, 1408], P('ep')
- ex_down: bfloat16 [64, 1408, 2048], P('ep')
Outputs:
- output 1: bfloat16 [2048, 2048], P(('dp', 'ep')), parts along dimension 0
- output 2: bfloat16 [2048, 64, 512], P(('dp', 'ep')), parts along dimension 0
- output 3: bfloat16 [2048, 64, 64], P(('dp', 'ep')), parts along dimension 0
There are 4 independent parts. A program takes and returns all parts, laid end to end along the dimension named above; an argument that names none is the same for every part.
All inputs are finite; a program needn't handle non-finite values.
Results may differ from a plain program's by a relative error of at most 0.0130062.
Values are sent between devices in bfloat16 or wider.
A program may use at most 768 MiB of HBM per device.

v0:
```python
import jax
import jax.numpy as jnp
from jax import lax
from jax.sharding import PartitionSpec as P

ROUTE_SCALE = 2.827
ROPE_BASE = 10000.0
NORM_EPS = 1e-6


def unit_norm(values):
    mean_sq = jnp.mean(jnp.square(values), axis=-1, keepdims=True)
    return values * lax.rsqrt(mean_sq + NORM_EPS)


def rms_norm(values, gain_vec):
    return unit_norm(values) * gain_vec.astype(jnp.float32)


def rope_rotate(values, angle_rad):
    half_dim = values.shape[-1] // 2
    x_first = values[..., :half_dim]
    x_second = values[..., half_dim:]
    cos_part = jnp.cos(angle_rad)
    sin_part = jnp.sin(angle_rad)
    return jnp.concatenate([x_first * cos_part - x_second * sin_part, x_second * cos_part + x_first * sin_part], axis=-1)


def attention_block(tok_in, lat_cache, rope_cache, tok_pos, attn_gain, w_query, w_kvdown, w_ukey, w_uval, w_out, ffn_gain):
    num_heads, nope_dim, kv_rank = w_ukey.shape
    rope_dim = rope_cache.shape[-1]
    seq_len = lat_cache.shape[1]
    tok_rows = tok_in.shape[0]
    x_wide = tok_in.astype(jnp.float32)
    x_norm = rms_norm(x_wide, attn_gain).astype(jnp.bfloat16)
    q_all = jnp.dot(x_norm, w_query, preferred_element_type=jnp.float32).astype(jnp.bfloat16).reshape(tok_rows, num_heads, nope_dim + rope_dim)
    kv_all = jnp.dot(x_norm, w_kvdown, preferred_element_type=jnp.float32)
    inv_freq = ROPE_BASE ** (-(2.0 * jnp.arange(rope_dim // 2)) / rope_dim)
    angle_rad = tok_pos.astype(jnp.float32)[:, None] * inv_freq[None, :]
    lat_new = unit_norm(kv_all[:, :kv_rank]).astype(jnp.bfloat16)
    rope_new = rope_rotate(kv_all[:, kv_rank:], angle_rad).astype(jnp.bfloat16)
    q_rope = rope_rotate(q_all[:, :, nope_dim:].astype(jnp.float32), angle_rad[:, None, :]).astype(jnp.bfloat16)
    q_lat = jnp.einsum('bhn,hnc->bhc', q_all[:, :, :nope_dim], w_ukey, preferred_element_type=jnp.float32).astype(jnp.bfloat16)
    seq_ids = jnp.arange(seq_len)
    at_pos = (seq_ids[None, :] == tok_pos[:, None])[:, :, None]
    lat_out = jnp.where(at_pos, lat_new[:, None, :], lat_cache)
    rope_out = jnp.where(at_pos, rope_new[:, None, :], rope_cache)
    scores = jnp.einsum('bhc,bsc->bhs', q_lat, lat_out, preferred_element_type=jnp.float32)
    scores = scores + jnp.einsum('bhr,bsr->bhs', q_rope, rope_out, preferred_element_type=jnp.float32)
    scores = scores * (nope_dim + rope_dim) ** -0.5
    visible = (seq_ids[None, :] <= tok_pos[:, None])[:, None, :]
    scores = jnp.where(visible, scores, -jnp.inf)
    prob_mat = jax.nn.softmax(scores, axis=-1).astype(jnp.bfloat16)
    o_lat = jnp.einsum('bhs,bsc->bhc', prob_mat, lat_out, preferred_element_type=jnp.float32).astype(jnp.bfloat16)
    o_heads = jnp.einsum('bhc,hcv->bhv', o_lat, w_uval, preferred_element_type=jnp.float32).astype(jnp.bfloat16)
    attn_out = jnp.dot(o_heads.reshape(tok_rows, -1), w_out, preferred_element_type=jnp.float32)
    resid_bf = (x_wide + attn_out).astype(jnp.bfloat16)
    h_norm = rms_norm(resid_bf.astype(jnp.float32), ffn_gain).astype(jnp.bfloat16)
    return resid_bf, h_norm, lat_out, rope_out


def route_weights(h_norm, w_router, expert_ids):
    num_experts = w_router.shape[1]
    gate_prob = jax.nn.sigmoid(jnp.dot(h_norm, w_router, preferred_element_type=jnp.float32))
    pick_mask = expert_ids[:, :, None] == jnp.arange(num_experts)[None, None, :]
    chosen = jnp.sum(jnp.where(pick_mask, gate_prob[:, None, :], 0.0), axis=-1)
    route_w = ROUTE_SCALE * chosen / jnp.sum(chosen, axis=1, keepdims=True)
    return route_w, pick_mask


def swiglu_shared(h_norm, sh_gate, sh_up, sh_down):
    gate_val = jnp.dot(h_norm, sh_gate, preferred_element_type=jnp.float32)
    up_val = jnp.dot(h_norm, sh_up, preferred_element_type=jnp.float32)
    act_val = (jax.nn.silu(gate_val) * up_val).astype(jnp.bfloat16)
    return jnp.dot(act_val, sh_down, preferred_element_type=jnp.float32)


def solution(mesh):
    ep_size = mesh.shape['ep']
    row_one = P(('dp', 'ep'))
    row_two = P(('dp', 'ep'), None)
    row_three = P(('dp', 'ep'), None, None)
    rep_one = P(None)
    rep_two = P(None, None)
    rep_three = P(None, None, None)
    exp_spec = P('ep', None, None)

    def local_step(tok_in, lat_cache, rope_cache, tok_pos, expert_ids, attn_gain, w_query, w_kvdown, w_ukey, w_uval, w_out, ffn_gain, w_router, sh_gate, sh_up, sh_down, ex_gate, ex_up, ex_down):
        resid_bf, h_norm, lat_out, rope_out = attention_block(tok_in, lat_cache, rope_cache, tok_pos, attn_gain, w_query, w_kvdown, w_ukey, w_uval, w_out, ffn_gain)
        route_w, pick_mask = route_weights(h_norm, w_router, expert_ids)
        shared_out = swiglu_shared(h_norm, sh_gate, sh_up, sh_down)
        tok_rows, top_k = expert_ids.shape
        num_experts = w_router.shape[1]
        local_experts = ex_gate.shape[0]
        d_model = h_norm.shape[1]
        cap_slots = max(2, -(-2 * tok_rows * top_k // num_experts))
        pick_int = pick_mask.astype(jnp.int32)
        per_tok = jnp.sum(pick_int, axis=1)
        before = jnp.cumsum(per_tok, axis=0) - per_tok
        slot_idx = jnp.sum(pick_int * before[:, None, :], axis=-1)
        slot_hot = slot_idx[:, :, None] == jnp.arange(cap_slots)
        place_hot = (pick_mask[:, :, :, None] & slot_hot[:, :, None, :]).astype(jnp.bfloat16)
        place_tok = jnp.sum(place_hot, axis=1)
        send_rows = jnp.einsum('tec,td->ecd', place_tok, h_norm, preferred_element_type=jnp.float32).astype(jnp.bfloat16)
        send_rows = send_rows.reshape(ep_size, local_experts, cap_slots, d_model)
        recv_rows = lax.all_to_all(send_rows, 'ep', 0, 2, tiled=True)
        recv_rows = recv_rows.reshape(local_experts, ep_size * cap_slots, d_model)
        gate_val = jnp.einsum('emd,edf->emf', recv_rows, ex_gate, preferred_element_type=jnp.float32)
        up_val = jnp.einsum('emd,edf->emf', recv_rows, ex_up, preferred_element_type=jnp.float32)
        act_val = (jax.nn.silu(gate_val) * up_val).astype(jnp.bfloat16)
        exp_out = jnp.einsum('emf,efd->emd', act_val, ex_down, preferred_element_type=jnp.float32).astype(jnp.bfloat16)
        exp_out = exp_out.reshape(1, local_experts, ep_size * cap_slots, d_model)
        back_rows = lax.all_to_all(exp_out, 'ep', 2, 0, tiled=True)
        back_rows = back_rows.reshape(num_experts, cap_slots, d_model)
        picked = jnp.einsum('tkec,ecd->tkd', place_hot, back_rows, preferred_element_type=jnp.float32)
        routed = jnp.sum(route_w[:, :, None] * picked, axis=1)
        out_hidden = (resid_bf.astype(jnp.float32) + shared_out + routed).astype(jnp.bfloat16)
        return out_hidden, lat_out, rope_out

    in_specs = (row_two, row_three, row_three, row_one, row_two, rep_one, rep_two, rep_two, rep_three, rep_three, rep_two, rep_one, rep_two, rep_two, rep_two, rep_two, exp_spec, exp_spec, exp_spec)
    out_specs = (row_two, row_three, row_three)
    return jax.shard_map(local_step, mesh=mesh, in_specs=in_specs, out_specs=out_specs, check_vma=False)
```

profile of v0, /device:TPU:21, one launch (start us, length us, event | category | flops | bytes accessed | tf_op | source)
XLA Modules:
  0.0 179.8 jit_solution(14710113786787572763)
XLA Ops:
  0.6 0.9 convert_reduce_fusion
  1.6 0.8 iota_compare_fusion
  2.4 0.7 iota_compare_fusion.3
  3.8 0.7 convert_element_type.89
  4.5 1.0 fusion.34
  5.5 7.0 %convolution_convert_fusion = bf16[32,3072]{1,0:T(8,128)(2,1)S(1)} fusion(bf16[2048,3072]{1,0:T(8,128)(2,1)} %param.25, bf16[32,2048]{1,0:T(8,128)(2,1)} %param.19, f32[2048]{0:T(1024)S(1)} %convert_element_type.89, f32[32]{0:T(128)S(1)} %add_rsqrt_fusion.2), kind=kOutput, calls=%fused_computation.3 | convolution fusion | flops 403013632 | bytes 12918912 | tf_op jit(solution)/shard_map/dot_general | solution.py:36
  13.3 0.8 fusion.46
  18.4 1.8 convolution_convert_fusion.3
  20.2 2.4 %fusion.18 = bf16[16,4,8,128]{3,2,1,0:T(8,128)(2,1)S(1)} fusion(bf16[16,512,128]{2,1,0:T(8,128)(2,1)} %param.28, bf16[32,16,512]{2,1,0:T(8,128)(2,1)} %convolution_convert_fusion.3), kind=kOutput, calls=%fused_computation.31 | convolution fusion | flops 67174400 | bytes 2752512 | tf_op jit(solution)/shard_map/bhc,hcv->bhv/dot_general | solution.py:55
  22.5 5.0 %multiply_reduce_fusion = (f32[32]{0:T(128)S(1)}, f32[32,2048]{1,0:T(8,128)S(1)}) fusion(bf16[2048,2048]{1,0:T(8,128)(2,1)} %param.29, bf16[16,4,8,128]{3,2,1,0:T(8,128)(2,1)S(1)} %fusion.18, bf16[32,2048]{1,0:T(8,128)(2,1)S(1)} %copy-done.3), kind=kOutput, calls=%fused_computation.56 | convolution fusion | flops 268828640 | bytes 8913024 | tf_op jit(solution)/shard_map/dot_general | solution.py:56
  28.5 2.0 %reshape.200 = bf16[16,4,6,2048]{3,1,0,2:T(4,128)(2,1)} reshape(bf16[64,6,2048]{2,0,1:T(8,128)(2,1)S(1)} %convolution_convert_fusion.2) | data formatting | bytes 3145728 | tf_op jit(solution)/shard_map/reshape | solution.py:105
  30.5 2.1 %copy.33 = bf16[16,4,6,2048]{3,1,2,0:T(4,128)(2,1)S(1)} copy(bf16[16,4,6,2048]{3,1,0,2:T(4,128)(2,1)} %reshape.200) | data formatting | bytes 3145728 | tf_op jit(solution)/shard_map/reshape | solution.py:105
  32.6 50.2 %all_to_all.30 = bf16[16,4,6,2048]{3,1,2,0:T(4,128)(2,1)S(1)} all-to-all(bf16[16,4,6,2048]{3,1,2,0:T(4,128)(2,1)S(1)} %copy.33), channel_id=1, replica_groups=mesh['dp'=4,'ep'=16] {'ep'}, dimensions={0} | all-to-all | bytes 3145728 | tf_op jit(solution)/shard_map/all_to_all | solution.py:106
  82.8 10.1 %fusion.10 = f32[4,96,1408]{2,1,0:T(8,128)S(1)} fusion(bf16[4,2048,1408]{2,1,0:T(8,128)(2,1)} %param.35, bf16[4,96,2048]{2,0,1:T(4,128)(2,1)S(1)} %bitcast.54), kind=kOutput, calls=%fused_computation.19 | convolution fusion | flops 2214592512 | bytes 26804224 | tf_op jit(solution)/shard_map/emd,edf->emf/dot_general | solution.py:108
  92.9 12.7 %fusion.2 = bf16[4,96,1408]{2,1,0:T(8,128)(2,1)S(1)} fusion(bf16[4,2048,1408]{2,1,0:T(8,128)(2,1)} %param.36, f32[4,96,1408]{2,1,0:T(8,128)S(1)} %fusion.10, bf16[4,96,2048]{2,0,1:T(4,128)(2,1)S(1)} %bitcast.55), kind=kOutput, calls=%fused_computation.7 | convolution fusion | flops 2217836544 | bytes 27885568 | tf_op jit(solution)/shard_map/emd,edf->emf/dot_general | solution.py:109
  105.6 11.6 %fusion.4 = bf16[1,4,96,2048]{3,2,1,0:T(8,128)(2,1)S(1)} fusion(bf16[4,96,1408]{2,1,0:T(8,128)(2,1)S(1)} %fusion.2, bf16[4,1408,2048]{2,1,0:T(8,128)(2,1)} %param.37), kind=kOutput, calls=%fused_computation.10 | convolution fusion | flops 2215378944 | bytes 25722880 | tf_op jit(solution)/shard_map/emf,efd->emd/dot_general | solution.py:111
  117.2 2.4 %copy.36 = bf16[1,4,96,2048]{3,1,0,2:T(4,128)(2,1)} copy(bf16[1,4,96,2048]{3,2,1,0:T(8,128)(2,1)S(1)} %fusion.4) | data formatting | bytes 3145728 | tf_op jit(solution)/shard_map/reshape | solution.py:112
  119.5 4.2 %all-to-all-start.1 = ((bf16[1,4,96,2048]{3,1,0,2:T(4,128)(2,1)}), bf16[1,4,96,2048]{3,1,0,2:T(4,128)(2,1)S(1)}, u32[]{:S(2)}, u32[]{:S(2)}) async-start(bf16[1,4,96,2048]{3,1,0,2:T(4,128)(2,1)} %copy.36), calls=%async_computation.1 | async-start | bytes 3145728 | tf_op jit(solution)/shard_map/all_to_all | solution.py:113
  124.3 6.4 %fusion.52 = f32[32,2816]{1,0:T(8,128)S(1)} fusion(bf16[2048,2816]{1,0:T(8,128)(2,1)} %param.32, f32[32,2048]{1,0:T(8,128)S(1)} %get-tuple-element.16, f32[2048]{0:T(1024)S(1)} %convert_element_type.104, f32[32]{0:T(128)S(1)} %add_rsqrt_fusion), kind=kOutput, calls=%fused_computation.94 | convolution fusion | flops 369295360 | bytes 12165248 | tf_op jit(solution)/shard_map/dot_general | solution.py:72
  130.7 31.4 %all-to-all-done.1 = bf16[1,4,96,2048]{3,1,0,2:T(4,128)(2,1)S(1)} async-done(((bf16[1,4,96,2048]{3,1,0,2:T(4,128)(2,1)}), bf16[1,4,96,2048]{3,1,0,2:T(4,128)(2,1)S(1)}, u32[]{:S(2)}, u32[]{:S(2)}) %all-to-all-start.1) | async-done | bytes 1572896 | tf_op jit(solution)/shard_map/all_to_all | solution.py:113
  162.1 2.1 %copy.37 = bf16[16,1,4,6,2048]{4,2,0,3,1:T(4,128)(2,1)} copy(bf16[16,1,4,6,2048]{4,2,3,0,1:T(4,128)(2,1)S(1)} %bitcast.56) | data formatting | bytes 3145728 | tf_op jit(solution)/shard_map/all_to_all | solution.py:113
  164.2 2.3 %reshape.205 = bf16[64,6,2048,1]{2,0,1,3:T(8,128)(2,1)S(1)} reshape(bf16[16,1,4,6,2048]{4,2,0,3,1:T(4,128)(2,1)} %copy.37) | data formatting | bytes 3145728 | tf_op jit(solution)/shard_map/reshape | solution.py:114
  166.5 0.8 fusion.12
  167.3 12.5 %fusion.6 = bf16[32,2048]{1,0:T(8,128)(2,1)} fusion(f32[32,2048]{1,0:T(8,128)S(1)} %fusion.12, f32[32,2048]{1,0:T(8,128)S(1)} %get-tuple-element.16, bf16[2816,2048]{1,0:T(8,128)(2,1)} %param.34, bf16[2048,2816]{1,0:T(8,128)(2,1)} %param.33, f32[32,2816]{1,0:T(8,128)S(1)} %fusion.52, f32[2048]{0:T(1024)S(1)} %convert_element_type.104, f32[32]{0:T(128)S(1)} %add_rsqrt_fusion), kind=kOutput, calls=%fused_computation.14 | convolution fusion | flops 739131392 | bytes 24092800 | tf_op jit(solution)/shard_map/dot_general | solution.py:75
  (51 shorter events, 7.0 us)
Async XLA Ops:
  0.6 12.7 %copy-start = (bf16[2048,576]{0,1:T(8,128)(2,1)S(1)}, bf16[2048,576]{0,1:T(8,128)(2,1)}, u32[]{:S(2)}) copy-start(bf16[2048,576]{0,1:T(8,128)(2,1)} %param.26) | copy-start | bytes 7077892
  5.5 7.5 %copy-start.9 = (s32[32,6]{0,1:T(8,128)S(1)}, s32[32,6]{0,1:T(8,128)}, u32[]{:S(2)}) copy-start(s32[32,6]{0,1:T(8,128)} %param.23) | copy-start | bytes 2308
  5.5 7.8 %copy-start.3 = (bf16[32,2048]{1,0:T(8,128)(2,1)S(1)}, bf16[32,2048]{1,0:T(8,128)(2,1)}, u32[]{:S(2)}) copy-start(bf16[32,2048]{1,0:T(8,128)(2,1)} %param.19) | copy-start | bytes 393220
  13.0 1.6 copy-start.5
  13.3 2.0 %copy-start.4 = (bf16[32,64,512]{2,1,0:T(8,128)(2,1)S(1)}, bf16[32,64,512]{2,1,0:T(8,128)(2,1)}, u32[]{:S(2)}) copy-start(bf16[32,64,512]{2,1,0:T(8,128)(2,1)} %param.20) | copy-start | bytes 6291460
  15.7 2.7 %copy-start.2 = (bf16[32,64,512]{2,1,0:T(8,128)(2,1)}, bf16[32,64,512]{2,1,0:T(8,128)(2,1)S(1)}, u32[]{:S(2)}) copy-start(bf16[32,64,512]{2,1,0:T(8,128)(2,1)S(1)} %broadcast_select_fusion) | copy-start | bytes 6291460
  15.7 1.4 copy-start.7
  17.5 2.7 %copy-start.6 = (bf16[32,64,64]{2,1,0:T(8,128)(2,1)}, bf16[32,64,64]{2,1,0:T(8,128)(2,1)S(1)}, u32[]{:S(2)}) copy-start(bf16[32,64,64]{2,1,0:T(8,128)(2,1)S(1)} %broadcast_select_fusion.1) | copy-start | bytes 786436
  17.7 2.5 %copy-start.10 = (bf16[2048]{0:T(1024)(128)(2,1)S(1)}, bf16[2048]{0:T(1024)(128)(2,1)}, u32[]{:S(2)}) copy-start(bf16[2048]{0:T(1024)(128)(2,1)} %param.30) | copy-start | bytes 12292
  119.5 4.2 %copy-start.8 = (bf16[2048,64]{0,1:T(8,128)(2,1)S(1)}, bf16[2048,64]{0,1:T(8,128)(2,1)}, u32[]{:S(2)}) copy-start(bf16[2048,64]{0,1:T(8,128)(2,1)} %param.31) | copy-start | bytes 786436
  119.5 42.5 %all-to-all-start.1 = ((bf16[1,4,96,2048]{3,1,0,2:T(4,128)(2,1)}), bf16[1,4,96,2048]{3,1,0,2:T(4,128)(2,1)S(1)}, u32[]{:S(2)}, u32[]{:S(2)}) async-start(bf16[1,4,96,2048]{3,1,0,2:T(4,128)(2,1)} %copy.36), calls=%async_computation.1 | async-start | bytes 3145728 | tf_op jit(solution)/shard_map/all_to_all | solution.py:113
  167.3 12.5 %copy-start.1 = (bf16[2048,576]{0,1:T(8,128)(2,1)S(1)}, bf16[2048,576]{0,1:T(8,128)(2,1)}, u32[]{:S(2)}) copy-start(bf16[2048,576]{0,1:T(8,128)(2,1)} %param.26) | copy-start | bytes 7077892
where the time goes:
time: 180 us
  matrix products  73.4 us (41%)
  blocking collectives  50.2 us (28%)
  waiting for transfers between devices  31.4 us (17%)
  local copies, waits for them, and re-layouts  12.4 us (7%)
  other arithmetic  7.28 us (4%)
  starting transfers between devices  4.22 us (2%)
    all_to_all x1, blocking collectives, local_step(): recv_rows = lax.all_to_all(send_rows, 'ep', 0, 2, tiled=True)  50.2 us
    all_to_all x1, waiting for transfers between devices, local_step(): back_rows = lax.all_to_all(exp_out, 'ep', 2, 0, tiled=True)  31.4 us
    dot_general x1, matrix products, local_step(): jnp.einsum('emd,edf->emf', recv_rows, ex_up, preferred_element_type=jnp.f...  12.7 us
    dot_general x1, matrix products, swiglu_shared(): return jnp.dot(act_val, sh_down, preferred_element_type=jnp.float32)  12.5 us
    dot_general x1, matrix products, local_step(): jnp.einsum('emf,efd->emd', act_val, ex_down, preferred_element_type=jnp.f...  11.6 us
    dot_general x1, matrix products, local_step(): jnp.einsum('emd,edf->emf', recv_rows, ex_gate, preferred_element_type=jnp...  10.1 us
    dot_general x1, matrix products, attention_block(): jnp.dot(x_norm, w_query, preferred_element_type=jnp.float32)  7.01 us
    dot_general x1, matrix products, swiglu_shared(): gate_val = jnp.dot(h_norm, sh_gate, preferred_element_type=jnp.float32)  6.42 us
  transfers between devices with their start and end apart: 1, of which 1 were waited for; matrix products, arithmetic and copies ran while one was open for 4% of the time, Pallas kernels for 0%

commit v1 on v0

v1 whole, which is shorter than its diff:
```python
import functools

import jax
import jax.numpy as jnp
import numpy as np
from jax import lax
from jax.experimental import pallas as pl
from jax.experimental.pallas import tpu as pltpu
from jax.sharding import PartitionSpec as P

ROUTE_SCALE = 2.827
ROPE_BASE = 10000.0
NORM_EPS = 1e-6
MESH = pl.DeviceIdType.MESH
F32 = jnp.float32
BF16 = jnp.bfloat16
CHUNKS = 4
SLOTS_A = 6
SLOTS_B = 8
CAP = 6
LANES = 128


def unit_norm(values):
    mean_sq = jnp.mean(jnp.square(values), axis=-1, keepdims=True)
    return values * lax.rsqrt(mean_sq + NORM_EPS)


def rms_norm(values, gain_vec):
    return unit_norm(values) * gain_vec.astype(jnp.float32)


def rope_rotate(values, angle_rad):
    half_dim = values.shape[-1] // 2
    x_first = values[..., :half_dim]
    x_second = values[..., half_dim:]
    cos_part = jnp.cos(angle_rad)
    sin_part = jnp.sin(angle_rad)
    return jnp.concatenate([x_first * cos_part - x_second * sin_part, x_second * cos_part + x_first * sin_part], axis=-1)


def attention_block(tok_in, lat_cache, rope_cache, tok_pos, attn_gain, w_query, w_kvdown, w_ukey, w_uval, w_out, ffn_gain):
    num_heads, nope_dim, kv_rank = w_ukey.shape
    rope_dim = rope_cache.shape[-1]
    seq_len = lat_cache.shape[1]
    tok_rows = tok_in.shape[0]
    x_wide = tok_in.astype(jnp.float32)
    x_norm = rms_norm(x_wide, attn_gain).astype(jnp.bfloat16)
    q_all = jnp.dot(x_norm, w_query, preferred_element_type=jnp.float32).astype(jnp.bfloat16).reshape(tok_rows, num_heads, nope_dim + rope_dim)
    kv_all = jnp.dot(x_norm, w_kvdown, preferred_element_type=jnp.float32)
    inv_freq = ROPE_BASE ** (-(2.0 * jnp.arange(rope_dim // 2)) / rope_dim)
    angle_rad = tok_pos.astype(jnp.float32)[:, None] * inv_freq[None, :]
    lat_new = unit_norm(kv_all[:, :kv_rank]).astype(jnp.bfloat16)
    rope_new = rope_rotate(kv_all[:, kv_rank:], angle_rad).astype(jnp.bfloat16)
    q_rope = rope_rotate(q_all[:, :, nope_dim:].astype(jnp.float32), angle_rad[:, None, :]).astype(jnp.bfloat16)
    q_lat = jnp.einsum('bhn,hnc->bhc', q_all[:, :, :nope_dim], w_ukey, preferred_element_type=jnp.float32).astype(jnp.bfloat16)
    seq_ids = jnp.arange(seq_len)
    at_pos = (seq_ids[None, :] == tok_pos[:, None])[:, :, None]
    lat_out = jnp.where(at_pos, lat_new[:, None, :], lat_cache)
    rope_out = jnp.where(at_pos, rope_new[:, None, :], rope_cache)
    scores = jnp.einsum('bhc,bsc->bhs', q_lat, lat_out, preferred_element_type=jnp.float32)
    scores = scores + jnp.einsum('bhr,bsr->bhs', q_rope, rope_out, preferred_element_type=jnp.float32)
    scores = scores * (nope_dim + rope_dim) ** -0.5
    visible = (seq_ids[None, :] <= tok_pos[:, None])[:, None, :]
    scores = jnp.where(visible, scores, -jnp.inf)
    prob_mat = jax.nn.softmax(scores, axis=-1).astype(jnp.bfloat16)
    o_lat = jnp.einsum('bhs,bsc->bhc', prob_mat, lat_out, preferred_element_type=jnp.float32).astype(jnp.bfloat16)
    o_heads = jnp.einsum('bhc,hcv->bhv', o_lat, w_uval, preferred_element_type=jnp.float32).astype(jnp.bfloat16)
    attn_out = jnp.dot(o_heads.reshape(tok_rows, -1), w_out, preferred_element_type=jnp.float32)
    resid_bf = (x_wide + attn_out).astype(jnp.bfloat16)
    h_norm = rms_norm(resid_bf.astype(jnp.float32), ffn_gain).astype(jnp.bfloat16)
    return resid_bf, h_norm, lat_out, rope_out


def route_table(h_norm, w_router, expert_ids):
    num_experts = w_router.shape[1]
    tok_rows = expert_ids.shape[0]
    gate_prob = jax.nn.sigmoid(jnp.dot(h_norm, w_router, preferred_element_type=jnp.float32))
    listed = jnp.sum((expert_ids[:, :, None] == jnp.arange(num_experts)[None, None, :]).astype(F32), axis=1)
    chosen = gate_prob * listed
    weights = ROUTE_SCALE * chosen / jnp.sum(chosen, axis=1, keepdims=True)
    earlier = jnp.tril(jnp.ones((tok_rows, tok_rows), F32))
    slots = jnp.dot(earlier, listed, preferred_element_type=F32) * listed
    return jnp.concatenate([weights, slots], axis=1)


def dot32(lhs, rhs):
    return jnp.dot(lhs, rhs, preferred_element_type=F32)


def wide_tiles(total, width):
    return [(start, min(width, total - start)) for start in range(0, total, width)]


def moe_kernel(n_ep, n_exp, h_ref, table_ref, resid_ref, rowpat_ref, colpat_ref,
               sg_ref, su_ref, sd_ref, eg_ref, eu_ref, ed_ref, out_ref,
               hall, gall, xg, act, act_sh, ebuf, esib, cmat, ct, ring, wa, wb, sh_out,
               sem_a, sem_b, ag_send, ag_recv, sib_send, sib_recv, tb_send, tb_recv, ts_send, ts_recv,
               ex_send, ex_recv, rg_send, rg_recv):
    nz = n_ep // 2
    far = nz // 2
    tok, dim = h_ref.shape
    e_loc, _, ff = eg_ref.shape
    halves = sg_ref.shape[1] // ff
    rows_par = nz * CAP
    rows_exp = 2 * rows_par
    rows_all = e_loc * rows_exp
    rows_q = e_loc * rows_par
    cw = dim // CHUNKS
    half_dim = dim // 2

    me = lax.axis_index('ep')
    z = me // 2
    par = lax.rem(me, 2)
    sib = me + 1 - 2 * par
    up_dev = lax.rem(z + 1, nz) * 2 + par
    dn_dev = lax.rem(z + nz - 1, nz) * 2 + par

    def chip(step):
        return lax.rem(z + step + 2 * nz, nz)

    def slot_of(p, zz):
        return p * nz + zz

    total_a = 2 * e_loc + 2 * halves

    def a_copy(unit, expert=None):
        slot = unit % SLOTS_A
        if unit < 2 * e_loc:
            src = (eg_ref if unit % 2 == 0 else eu_ref).at[unit // 2]
        else:
            hf = (unit - 2 * e_loc) // 2
            src = (sg_ref if unit % 2 == 0 else su_ref).at[:, pl.ds(hf * ff, ff)]
        return pltpu.make_async_copy(src, wa.at[slot], sem_a.at[slot])

    total_b = CHUNKS * (e_loc + halves)

    def b_copy(unit):
        slot = unit % SLOTS_B
        if unit < CHUNKS * e_loc:
            j, e = unit // e_loc, unit % e_loc
            src = ed_ref.at[e, :, pl.ds(j * cw, cw)]
        else:
            j, hf = (unit - CHUNKS * e_loc) // halves, (unit - CHUNKS * e_loc) % halves
            src = sd_ref.at[pl.ds(hf * ff, ff), pl.ds(j * cw, cw)]
        return pltpu.make_async_copy(src, wb.at[slot], sem_b.at[slot])

    for unit in range(min(SLOTS_A, total_a)):
        a_copy(unit).start()

    barrier = pltpu.get_barrier_semaphore()
    for dev in (up_dev, dn_dev, sib):
        pl.semaphore_signal(barrier, inc=1, device_id={'ep': dev}, device_id_type=MESH)
    pl.semaphore_wait(barrier, 3)

    def remote(src, dst, send, recv, dev):
        return pltpu.make_async_remote_copy(src_ref=src, dst_ref=dst, send_sem=send, recv_sem=recv,
                                            device_id={'ep': dev}, device_id_type=MESH)

    def h_hop(way, step):
        dev = up_dev if way == 0 else dn_dev
        origin = chip(-step if way == 0 else step)
        slot = slot_of(par, origin)
        if step == far - 1:
            cols = pl.ds(way * half_dim, half_dim)
            src, dst = hall.at[slot, :, cols], hall.at[slot, :, cols]
        else:
            src = h_ref if step == 0 else hall.at[slot]
            dst = hall.at[slot]
        return remote(src, dst, ag_send.at[way, step], ag_recv.at[way, step], dev)

    def t_hop(way, step):
        dev = up_dev if way == 0 else dn_dev
        origin = chip(-step if way == 0 else step)
        slot = slot_of(par, origin)
        src = table_ref if step == 0 else gall.at[slot]
        return remote(src, gall.at[slot], tb_send.at[way, step], tb_recv.at[way, step], dev)

    def h_cross(k, origin):
        slot = slot_of(par, origin)
        src = h_ref if k == 0 else hall.at[slot]
        return remote(src, hall.at[slot], sib_send.at[k], sib_recv.at[k], sib)

    def t_cross(k, origin):
        slot = slot_of(par, origin)
        src = table_ref if k == 0 else gall.at[slot]
        return remote(src, gall.at[slot], ts_send.at[k], ts_recv.at[k], sib)

    t_steps = (far, far - 1)
    sent = []

    def go(copy):
        copy.start()
        sent.append(copy)
        return copy

    hops = [[None] * far, [None] * far]
    thops = [[None] * far, [None] * far]
    for way in range(2):
        thops[way][0] = go(t_hop(way, 0))
        hops[way][0] = go(h_hop(way, 0))
    crossed = [go(t_cross(0, z)), go(h_cross(0, z))]
    hall[slot_of(par, z)] = h_ref[...]
    gall[slot_of(par, z)] = table_ref[...]
    k = 1
    for step in range(far):
        for way in range(2):
            origin = chip(-(step + 1) if way == 0 else step + 1)
            if step < t_steps[way]:
                thops[way][step].wait_recv()
                if step + 1 < t_steps[way]:
                    thops[way][step + 1] = go(t_hop(way, step + 1))
                crossed.append(go(t_cross(k if step < far - 1 else 2 * far - 1, origin)))
            hops[way][step].wait_recv()
            if step + 1 < far:
                hops[way][step + 1] = go(h_hop(way, step + 1))
                crossed.append(go(h_cross(k, origin)))
                k += 1
    crossed.append(go(h_cross(2 * far - 1, chip(far))))
    for copy in crossed:
        copy.wait_recv()

    rowpat = rowpat_ref[...]
    row_exp, row_dev, row_slot = rowpat[:, 0:1], rowpat[:, 1:2], rowpat[:, 2:3]
    base = n_exp + e_loc * me
    lane = lax.broadcasted_iota(jnp.int32, (rows_all, LANES), 1)
    pick = jnp.where(lane == base + row_exp.astype(jnp.int32), 1.0, 0.0).astype(BF16)
    slots_by_row = lax.dot_general(pick, gall[...].reshape(n_ep * tok, LANES).astype(BF16), (((1,), (1,)), ((), ())),
                                   preferred_element_type=F32)
    tok_dev = (lax.broadcasted_iota(jnp.int32, (rows_all, n_ep * tok), 1) // tok).astype(F32)
    place = jnp.where((slots_by_row == row_slot) & (tok_dev == row_dev), 1.0, 0.0).astype(BF16)
    for start, width in wide_tiles(dim, 256):
        rows = hall[:, :, start:start + width].reshape(n_ep * tok, width)
        xg[:, :, start:start + width] = dot32(place, rows).astype(BF16).reshape(e_loc, rows_exp, width)

    colpat = colpat_ref[...]
    col_exp, col_chip, col_slot = colpat[0:1, :], colpat[1:2, :], colpat[2:3, :]
    g_own = gall[pl.ds(par * nz, nz)].reshape(nz * tok, LANES)
    part1 = g_own.astype(BF16)
    rest1 = g_own - part1.astype(F32)
    part2 = rest1.astype(BF16)
    part3 = (rest1 - part2.astype(F32)).astype(BF16)
    sub = lax.broadcasted_iota(jnp.int32, (LANES, rows_q), 0)
    tok_chip = (lax.broadcasted_iota(jnp.int32, (nz * tok, rows_q), 0) // tok).astype(F32)
    for q in range(2):
        ids = e_loc * (me if q == 0 else sib) + col_exp.astype(jnp.int32)
        sel_w = jnp.where(sub == ids, 1.0, 0.0).astype(BF16)
        sel_s = jnp.where(sub == n_exp + ids, 1.0, 0.0).astype(BF16)
        here = (dot32(part1, sel_s) == col_slot) & (tok_chip == col_chip)
        for i, part in enumerate((part1, part2, part3)):
            cmat[q, i] = jnp.where(here, dot32(part, sel_w), 0.0).astype(BF16)

    def swiglu_tiles(x, slot_g, slot_u, store):
        for start, width in wide_tiles(ff, 256):
            gate = dot32(x, wa[slot_g, :, start:start + width])
            up = dot32(x, wa[slot_u, :, start:start + width])
            store(start, width, (jax.nn.silu(gate) * up).astype(BF16))

    def wait_a(slot):
        pltpu.make_async_copy(eg_ref.at[0], wa.at[slot], sem_a.at[slot]).wait()

    def wait_b(slot):
        pltpu.make_async_copy(ed_ref.at[0, :, pl.ds(0, cw)], wb.at[slot], sem_b.at[slot]).wait()

    def expert_up(e, carry):
        slot_g = lax.rem(2 * e, SLOTS_A)
        slot_u = lax.rem(2 * e + 1, SLOTS_A)
        wait_a(slot_g)
        wait_a(slot_u)

        def store(start, width, val):
            act[e, :, start:start + width] = val
        swiglu_tiles(xg[e], slot_g, slot_u, store)
        for e_st in range(e_loc):
            @pl.when(e == e_st)
            def _():
                for unit in (2 * e_st + SLOTS_A, 2 * e_st + 1 + SLOTS_A):
                    if unit < 2 * e_loc:
                        a_copy(unit).start()
                if e_st == 0:
                    for unit in range(SLOTS_B):
                        b_copy(unit).start()
                for unit in (2 * e_st + SLOTS_A, 2 * e_st + 1 + SLOTS_A):
                    if 2 * e_loc <= unit < total_a:
                        a_copy(unit).start()
        return carry

    lax.fori_loop(0, e_loc, expert_up, 0)

    def reach(way, j):
        return far if (way + j) % 2 == 0 else nz - 1 - far

    def ring_copy(way, j, step):
        dev = up_dev if way == 0 else dn_dev
        ahead = reach(way, j) - step + 1
        dest = chip(ahead if way == 0 else -ahead)
        src = ct.at[j, dest] if step == 1 else ring.at[way, j, step - 2]
        return remote(src, ring.at[way, j, step - 1], rg_send.at[way, j, step - 1], rg_recv.at[way, j, step - 1], dev)

    rcopies = {}

    def combine(j):
        exch[j].wait_recv()
        own = ebuf[j, par].reshape(rows_q, cw)
        other = esib[j].reshape(rows_q, cw)
        for start, width in wide_tiles(cw, 256):
            total = dot32(cmat[0, 0], own[:, start:start + width]) + dot32(cmat[1, 0], other[:, start:start + width])
            for i in (1, 2):
                total += dot32(cmat[0, i], own[:, start:start + width]) + dot32(cmat[1, i], other[:, start:start + width])
            ct[j, :, :, start:start + width] = total.reshape(nz, tok, width)
        for way in range(2):
            rcopies[way, j, 1] = go(ring_copy(way, j, 1))

    def advance(j, step):
        for way in range(2):
            if step < reach(way, j):
                rcopies[way, j, step].wait_recv()
                ahead = reach(way, j) - step
                dest = chip(ahead if way == 0 else -ahead)
                ring[way, j, step - 1] += ct[j, dest]
                rcopies[way, j, step + 1] = go(ring_copy(way, j, step + 1))

    def finish(j):
        cols = slice(j * cw, (j + 1) * cw)
        total = resid_ref[:, cols].astype(F32) + sh_out[:, cols] + ct[j, z]
        for way in range(2):
            rcopies[way, j, reach(way, j)].wait_recv()
            total += ring[way, j, reach(way, j) - 1]
        out_ref[:, cols] = total.astype(BF16)

    exch = {}

    def down(j):
        def one(e, carry):
            slot = lax.rem(j * e_loc + e, SLOTS_B)
            wait_b(slot)
            res = dot32(act[e], wb[slot]).astype(BF16)
            ebuf[j, 0, e] = res[:rows_par]
            ebuf[j, 1, e] = res[rows_par:]
            return carry
        lax.fori_loop(0, e_loc, one, 0)
        for e in range(e_loc):
            unit = j * e_loc + e + SLOTS_B
            if unit < total_b:
                b_copy(unit).start()
        exch[j] = go(remote(ebuf.at[j, 1 - par], esib.at[j], ex_send.at[j], ex_recv.at[j], sib))

    def shared_up(hf):
        unit = 2 * e_loc + 2 * hf
        wait_a(unit % SLOTS_A)
        wait_a((unit + 1) % SLOTS_A)

        def store(start, width, val):
            act_sh[hf, :, start:start + width] = val
        swiglu_tiles(h_ref[...], unit % SLOTS_A, (unit + 1) % SLOTS_A, store)

    def shared_down(j):
        total = jnp.zeros((tok, cw), F32)
        for hf in range(halves):
            unit = CHUNKS * e_loc + j * halves + hf
            wait_b(unit % SLOTS_B)
            total += dot32(act_sh[hf], wb[unit % SLOTS_B])
        sh_out[:, j * cw:(j + 1) * cw] = total
        for hf in range(halves):
            unit = CHUNKS * e_loc + j * halves + hf + SLOTS_B
            if unit < total_b:
                b_copy(unit).start()

    down(0)
    down(1)
    combine(0)
    down(2)
    combine(1)
    advance(0, 1)
    down(3)
    combine(2)
    advance(1, 1)
    combine(3)
    advance(0, 2)
    shared_up(0)
    advance(2, 1)
    advance(1, 2)
    advance(3, 1)
    shared_up(1)
    advance(0, 3)
    advance(2, 2)
    shared_down(0)
    advance(1, 3)
    advance(3, 2)
    shared_down(1)
    advance(2, 3)
    shared_down(2)
    advance(3, 3)
    shared_down(3)
    for j in range(CHUNKS):
        finish(j)
    for copy in sent:
        copy.wait_send()


def moe_call(n_ep, h_norm, table, resid, w_sg, w_su, w_sd, w_eg, w_eu, w_ed):
    nz = n_ep // 2
    tok, dim = h_norm.shape
    e_loc, _, ff = w_eg.shape
    n_exp = e_loc * n_ep
    halves = w_sg.shape[1] // ff
    far = nz // 2
    cw = dim // CHUNKS
    rows_par = nz * CAP
    rows_exp = 2 * rows_par
    rows_all = e_loc * rows_exp
    rows_q = e_loc * rows_par
    row = np.arange(rows_all)
    rowpat = np.zeros((rows_all, 8), np.float32)
    rowpat[:, 0] = row // rows_exp
    rowpat[:, 1] = (row % rows_exp) // CAP
    rowpat[:, 2] = row % CAP + 1
    col = np.arange(rows_q)
    colpat = np.zeros((8, rows_q), np.float32)
    colpat[0] = col // rows_par
    colpat[1] = (col % rows_par) // CAP
    colpat[2] = col % CAP + 1
    vmem = pl.BlockSpec(memory_space=pltpu.VMEM)
    hbm = pl.BlockSpec(memory_space=pl.ANY)
    dma = pltpu.SemaphoreType.DMA
    return pl.pallas_call(
        functools.partial(moe_kernel, n_ep, n_exp),
        out_shape=jax.ShapeDtypeStruct((tok, dim), BF16),
        in_specs=[vmem] * 5 + [hbm] * 6,
        out_specs=vmem,
        scratch_shapes=[
            pltpu.VMEM((n_ep, tok, dim), BF16),
            pltpu.VMEM((n_ep, tok, LANES), F32),
            pltpu.VMEM((e_loc, rows_exp, dim), BF16),
            pltpu.VMEM((e_loc, rows_exp, ff), BF16),
            pltpu.VMEM((halves, tok, ff), BF16),
            pltpu.VMEM((CHUNKS, 2, e_loc, rows_par, cw), BF16),
            pltpu.VMEM((CHUNKS, e_loc, rows_par, cw), BF16),
            pltpu.VMEM((2, 3, nz * tok, rows_q), BF16),
            pltpu.VMEM((CHUNKS, nz, tok, cw), F32),
            pltpu.VMEM((2, CHUNKS, far, tok, cw), F32),
            pltpu.VMEM((SLOTS_A, dim, ff), BF16),
            pltpu.VMEM((SLOTS_B, ff, cw), BF16),
            pltpu.VMEM((tok, dim), F32),
            dma((SLOTS_A,)), dma((SLOTS_B,)),
            dma((2, far)), dma((2, far)), dma((nz,)), dma((nz,)),
            dma((2, far)), dma((2, far)), dma((nz,)), dma((nz,)),
            dma((CHUNKS,)), dma((CHUNKS,)),
            dma((2, CHUNKS, far)), dma((2, CHUNKS, far)),
        ],
        compiler_params=pltpu.CompilerParams(collective_id=0, has_side_effects=True, vmem_limit_bytes=67000000),
        name='moe_ring',
    )(h_norm, table, resid, jnp.asarray(rowpat), jnp.asarray(colpat), w_sg, w_su, w_sd, w_eg, w_eu, w_ed)


def solution(mesh):
    n_ep = mesh.shape['ep']
    row_one = P(('dp', 'ep'))
    row_two = P(('dp', 'ep'), None)
    row_three = P(('dp', 'ep'), None, None)
    rep_one = P(None)
    rep_two = P(None, None)
    rep_three = P(None, None, None)
    exp_spec = P('ep', None, None)

    def local_step(tok_in, lat_cache, rope_cache, tok_pos, expert_ids, attn_gain, w_query, w_kvdown, w_ukey, w_uval, w_out, ffn_gain, w_router, sh_gate, sh_up, sh_down, ex_gate, ex_up, ex_down):
        resid_bf, h_norm, lat_out, rope_out = attention_block(tok_in, lat_cache, rope_cache, tok_pos, attn_gain, w_query, w_kvdown, w_ukey, w_uval, w_out, ffn_gain)
        table = route_table(h_norm, w_router, expert_ids)
        out_hidden = moe_call(n_ep, h_norm, table, resid_bf, sh_gate, sh_up, sh_down, ex_gate, ex_up, ex_down)
        return out_hidden, lat_out, rope_out

    in_specs = (row_two, row_three, row_three, row_one, row_two, rep_one, rep_two, rep_two, rep_three, rep_three, rep_two, rep_one, rep_two, rep_two, rep_two, rep_two, exp_spec, exp_spec, exp_spec)
    out_specs = (row_two, row_three, row_three)
    return jax.shard_map(local_step, mesh=mesh, in_specs=in_specs, out_specs=out_specs, check_vma=False)
```

time: 180 us -> 104 us (0.58)
  Pallas kernels: 0 us -> 71.2 us
  matrix products: 73.4 us -> 22 us
  blocking collectives: 50.2 us -> 0 us
  waiting for transfers between devices: 31.4 us -> 0 us
  local copies, waits for them, and re-layouts: 12.4 us -> 4.12 us
  starting transfers between devices: 4.22 us -> 0 us
  other arithmetic: 7.28 us -> 5.25 us
    pallas_call x0 -> x1, Pallas kernels: none -> 71.2 us  [moe_call(): pl.pallas_call(functools.partial(moe_kernel, n_ep, n_exp), out_shape=jax....]
    dot_general x8 -> x2, matrix products: 54.9 us -> 0.44 us  [the longest x1 0.32 us: route_table(): jnp.dot(h_norm, w_router, preferred_element_type=jnp.float32)]
    all_to_all x1 -> x0, blocking collectives: 50.2 us -> none  [local_step(): recv_rows = lax.all_to_all(send_rows, 'ep', 0, 2, tiled=True)]
    all_to_all x1 -> x0, waiting for transfers between devices: 31.4 us -> none  [local_step(): back_rows = lax.all_to_all(exp_out, 'ep', 2, 0, tiled=True)]
    reshape x4 -> x0, local copies, waits for them, and re-layouts: 8.86 us -> none  [the longest x2 4.14 us: local_step(): send_rows = send_rows.reshape(ep_size, local_experts, cap_slots, d_model)]
    all_to_all x1 -> x0, starting transfers between devices: 4.22 us -> none  [local_step(): back_rows = lax.all_to_all(exp_out, 'ep', 2, 0, tiled=True)]
    unnamed x22 -> x23, local copies, waits for them, and re-layouts: 1.14 us -> 3.79 us
    all_to_all x1 -> x0, local copies, waits for them, and re-layouts: 2.11 us -> none  [local_step(): back_rows = lax.all_to_all(exp_out, 'ep', 2, 0, tiled=True)]
  transfers between devices with their start and end apart: 1 -> 0, of which waited for: 1 -> 0; matrix products, arithmetic and copies ran while one was open for 4% -> 0% of each run, Pallas kernels for 0% -> 0%
where the time goes in v1:
time: 104 us; the launch traced here: 103 us
  Pallas kernels  71.2 us (68%)
  matrix products  22 us (21%)
  other arithmetic  5.25 us (5%)
  local copies, waits for them, and re-layouts  4.12 us (4%)
    pallas_call x1, Pallas kernels, moe_call(): pl.pallas_call(functools.partial(moe_kernel, n_ep, n_exp), out_shape=jax....  71.2 us
    dot_general x1, matrix products, attention_block(): jnp.dot(x_norm, w_query, preferred_element_type=jnp.float32)  7.65 us
    dot_general x1, matrix products, attention_block(): jnp.dot(o_heads.reshape(tok_rows, -1), w_out, preferred_element_type=jnp....  5.08 us
    unnamed x23, local copies, waits for them, and re-layouts  3.79 us
    dot_general x1, matrix products, attention_block(): kv_all = jnp.dot(x_norm, w_kvdown, preferred_element_type=jnp.float32)  2.54 us
    dot_general x1, matrix products, attention_block(): jnp.einsum('bhc,hcv->bhv', o_lat, w_uval, preferred_element_type=jnp.floa...  2.21 us

profile of v1, /device:TPU:21, one launch (start us, length us, event | category | flops | bytes accessed | tf_op | source)
XLA Modules:
  0.0 103.5 jit_solution(17153325961024073777)
XLA Ops:
  0.6 0.9 iota_compare_fusion.3
  1.5 0.7 convert_element_type.68
  2.2 1.0 %fusion.18 = f32[32]{0:T(128)S(1)} fusion(bf16[32,2048]{1,0:T(8,128)(2,1)} %param.21), kind=kLoop, calls=%fused_computation.32 | loop fusion | flops 196576 | bytes 131200 | tf_op jit(solution)/shard_map/reduce_sum | solution.py:25
  3.3 2.5 %fusion.28 = f32[32,576]{1,0:T(8,128)S(1)} fusion(bf16[2048,576]{0,1:T(8,128)(2,1)} %param.28, bf16[32,2048]{1,0:T(8,128)(2,1)} %param.21, f32[2048]{0:T(1024)S(1)} %convert_element_type.68, f32[32]{0:T(128)S(1)} %add_rsqrt_fusion.2), kind=kOutput, calls=%fused_computation.50 | convolution fusion | flops 75759616 | bytes 2572416 | tf_op jit(solution)/shard_map/dot_general | solution.py:50
  6.0 0.5 broadcast_select_fusion
  6.5 0.4 copy-done.1
  6.9 7.7 %convolution_convert_fusion = bf16[32,3072]{1,0:T(8,128)(2,1)S(1)} fusion(bf16[2048,3072]{1,0:T(8,128)(2,1)} %param.27, bf16[32,2048]{1,0:T(8,128)(2,1)S(1)} %copy-done.1, f32[2048]{0:T(1024)S(1)} %convert_element_type.68, f32[32]{0:T(128)S(1)} %add_rsqrt_fusion.2), kind=kOutput, calls=%fused_computation.1 | convolution fusion | flops 403013632 | bytes 12918912 | tf_op jit(solution)/shard_map/dot_general | solution.py:49
  14.6 0.3 reshape.149
  14.9 2.0 %fusion.2 = bf16[32,16,512]{2,0,1:T(8,128)(2,1)S(1)} fusion(bf16[16,128,512]{2,1,0:T(8,128)(2,1)} %param.29, bf16[32,16,128]{2,1,0:T(8,128)(2,1)S(1)} %slice.31), kind=kOutput, calls=%fused_computation.7 | convolution fusion | flops 67371008 | bytes 2752512 | tf_op jit(solution)/shard_map/bhn,hnc->bhc/dot_general | solution.py:56
  17.0 0.7 fusion.13
  18.0 0.3 broadcast_select_fusion.1
  18.4 0.2 subtract_convert_fusion
  18.6 0.6 copy-done.3
  19.1 0.4 fusion.6
  19.6 0.2 fusion.38
  19.8 1.0 convolution_convert_fusion.1
  20.8 2.2 %fusion.7 = bf16[16,4,8,128]{3,2,1,0:T(8,128)(2,1)S(1)} fusion(bf16[16,512,128]{2,1,0:T(8,128)(2,1)} %param.30, bf16[32,16,512]{2,1,0:T(8,128)(2,1)S(1)} %convolution_convert_fusion.1), kind=kOutput, calls=%fused_computation.14 | convolution fusion | flops 67174400 | bytes 2752512 | tf_op jit(solution)/shard_map/bhc,hcv->bhv/dot_general | solution.py:68
  23.0 5.1 %fusion.15 = (f32[32]{0:T(128)S(1)}, bf16[32,2048]{1,0:T(8,128)(2,1)S(1)}) fusion(bf16[2048,2048]{1,0:T(8,128)(2,1)} %param.31, bf16[16,4,8,128]{3,2,1,0:T(8,128)(2,1)S(1)} %fusion.7, bf16[32,2048]{1,0:T(8,128)(2,1)S(1)} %copy-done.1), kind=kOutput, calls=%fused_computation.29 | convolution fusion | flops 268828640 | bytes 8781952 | tf_op jit(solution)/shard_map/dot_general | solution.py:69
  28.2 0.6 copy-done.4
  29.1 0.4 copy-done.5
  29.5 0.3 fusion.39
  29.9 0.7 pad_maximum_fusion.table_ref
  30.6 71.2 %moe_ring.1 = bf16[32,2048]{1,0:T(8,128)(2,1)} custom-call(bf16[32,2048]{1,0:T(8,128)(2,1)} %copy-done.5, f32[32,128]{1,0:T(8,128)} %pad_maximum_fusion.table_ref, bf16[32,2048]{1,0:T(8,128)(2,1)} %copy-done.4, f32[384,8]{1,0:T(8,128)} %constant.34.clone.rowpat_ref, f32[8,192]{1,0:T(8,128)} %constant.35.clone.colpat_ref, bf16[2048,2816]{1,0:T(8,128)(2,1)} %sg_ref.1, ...), custom_call_target="tpu_custom_call" | custom-call | tf_op jit(solution)/shard_map/moe_ring/pallas_call | solution.py:426
  101.9 1.6 %copy.46 = bf16[32,2048]{1,0:T(8,128)(2,1)} copy(bf16[32,2048]{1,0:T(8,128)(2,1)} %moe_ring.1) | data formatting | bytes 262144
  (34 shorter events, 1.1 us)
Async XLA Ops:
  0.6 5.4 %copy-start.2 = (bf16[32,64,512]{2,1,0:T(8,128)(2,1)S(1)}, bf16[32,64,512]{2,1,0:T(8,128)(2,1)}, u32[]{:S(2)}) copy-start(bf16[32,64,512]{2,1,0:T(8,128)(2,1)} %param.22) | copy-start | bytes 6291460
  6.0 0.9 copy-start.1
  6.9 12.9 %copy-start = (bf16[32,64,512]{2,1,0:T(8,128)(2,1)}, bf16[32,64,512]{2,1,0:T(8,128)(2,1)S(1)}, u32[]{:S(2)}) copy-start(bf16[32,64,512]{2,1,0:T(8,128)(2,1)S(1)} %broadcast_select_fusion) | copy-start | bytes 6291460
  16.9 0.7 copy-start.10
  16.9 1.1 %copy-start.6 = (bf16[32,64,64]{2,1,0:T(8,128)(2,1)S(1)}, bf16[32,64,64]{2,1,0:T(8,128)(2,1)}, u32[]{:S(2)}) copy-start(bf16[32,64,64]{2,1,0:T(8,128)(2,1)} %param.23) | copy-start | bytes 786436
  18.3 0.8 copy-start.3
  23.0 5.1 %copy-start.8 = (bf16[2048]{0:T(1024)(128)(2,1)S(1)}, bf16[2048]{0:T(1024)(128)(2,1)}, u32[]{:S(2)}) copy-start(bf16[2048]{0:T(1024)(128)(2,1)} %param.32) | copy-start | bytes 12292
  23.0 5.9 %copy-start.9 = (s32[32,6]{0,1:T(8,128)S(1)}, s32[32,6]{0,1:T(8,128)}, u32[]{:S(2)}) copy-start(s32[32,6]{0,1:T(8,128)} %param.25) | copy-start | bytes 2308
  23.0 6.5 %copy-start.7 = (bf16[2048,64]{0,1:T(8,128)(2,1)S(1)}, bf16[2048,64]{0,1:T(8,128)(2,1)}, u32[]{:S(2)}) copy-start(bf16[2048,64]{0,1:T(8,128)(2,1)} %param.33) | copy-start | bytes 786436
  28.1 0.6 copy-start.4
  28.9 0.7 copy-start.5

commit v2 on v1

v2 whole, which is shorter than its diff:
```python
import functools

import jax
import jax.numpy as jnp
import numpy as np
from jax import lax
from jax.experimental import pallas as pl
from jax.experimental.pallas import tpu as pltpu
from jax.sharding import PartitionSpec as P

ROUTE_SCALE = 2.827
ROPE_BASE = 10000.0
NORM_EPS = 1e-6
MESH = pl.DeviceIdType.MESH
F32 = jnp.float32
BF16 = jnp.bfloat16
CHUNKS = 4
SLOTS_A = 7
SLOTS_B = 4
CAP = 6
LANES = 128
GROUP = 4


def unit_norm(values):
    mean_sq = jnp.mean(jnp.square(values), axis=-1, keepdims=True)
    return values * lax.rsqrt(mean_sq + NORM_EPS)


def dot32(lhs, rhs):
    return jnp.dot(lhs, rhs, preferred_element_type=F32)


def wide_tiles(total, width):
    return [(start, min(width, total - start)) for start in range(0, total, width)]


def attn_kernel(pos_ref, x_ref, trig_ref, ids_ref, ag_ref, fg_ref, wq_ref, wkv_ref, uk_ref, uv_ref, wo_ref, wr_ref, lat_ref, rope_ref,
                res_ref, h_ref, table_ref, lat_out, rope_out,
                wq, wkv, uk, uv, wo, wr, lat, rope, q_lat, q_rope, o_lat, o_heads, sem_q, sem_w, sem_c, sem_o):
    n_heads, nope, rank = uk_ref.shape
    tok, dim = x_ref.shape
    seq, rope_dim = rope_ref.shape[1:]
    half = rope_dim // 2
    head = nope + rope_dim
    n_exp = wr_ref.shape[1]
    blocks = n_heads // GROUP
    q_cols = GROUP * head

    def q_copy(blk):
        return pltpu.make_async_copy(wq_ref.at[:, pl.ds(blk * q_cols, q_cols)], wq.at[blk], sem_q.at[blk])

    kv_copy = pltpu.make_async_copy(wkv_ref, wkv, sem_w.at[0])
    uk_copy = pltpu.make_async_copy(uk_ref, uk, sem_w.at[1])
    uv_copy = pltpu.make_async_copy(uv_ref, uv, sem_w.at[2])
    wo_copy = pltpu.make_async_copy(wo_ref, wo, sem_w.at[3])
    wr_copy = pltpu.make_async_copy(wr_ref, wr, sem_w.at[4])
    lat_copy = pltpu.make_async_copy(lat_ref, lat, sem_c.at[0])
    rope_copy = pltpu.make_async_copy(rope_ref, rope, sem_c.at[1])
    kv_copy.start()
    lat_copy.start()
    rope_copy.start()
    uk_copy.start()
    for blk in range(blocks):
        q_copy(blk).start()
    uv_copy.start()
    wr_copy.start()
    wo_copy.start()

    x = x_ref[...].astype(F32)
    x_norm = (unit_norm(x) * ag_ref[...].astype(F32)).astype(BF16)
    cos, sin = trig_ref[:, :half], trig_ref[:, half:]

    def rotate(first, second):
        return jnp.concatenate([first * cos - second * sin, second * cos + first * sin], axis=1)

    kv_copy.wait()
    kv = dot32(x_norm, wkv[...])
    lat_new = unit_norm(kv[:, :rank]).astype(BF16).astype(F32)
    rope_new = rotate(kv[:, rank:rank + half], kv[:, rank + half:]).astype(BF16).astype(F32)
    lat_copy.wait()
    rope_copy.wait()
    for t in range(tok):
        here = lax.broadcasted_iota(jnp.int32, (seq, rank), 0) == pos_ref[t]
        lat[t] = jnp.where(here, lat_new[t:t + 1], lat[t].astype(F32)).astype(BF16)
        here = lax.broadcasted_iota(jnp.int32, (seq, rope_dim), 0) == pos_ref[t]
        rope[t] = jnp.where(here, rope_new[t:t + 1], rope[t].astype(F32)).astype(BF16)
    lat_back = pltpu.make_async_copy(lat, lat_out, sem_o.at[0])
    rope_back = pltpu.make_async_copy(rope, rope_out, sem_o.at[1])

    def spread(ref, n, val):
        for c in range(val.shape[1] // LANES):
            ref[c, pl.ds(n, tok, stride=n_heads), :] = val[:, c * LANES:(c + 1) * LANES]

    uk_copy.wait()
    for blk in range(blocks):
        q_copy(blk).wait()
        q = dot32(x_norm, wq[blk]).astype(BF16)
        for i in range(GROUP):
            n = blk * GROUP + i
            at = i * head
            q_n = dot32(q[:, at:at + nope], uk[n]).astype(BF16).astype(F32)
            spread(q_lat, n, q_n)
            q_r = q[:, at + nope:at + head].astype(F32)
            q_r = rotate(q_r[:, :half], q_r[:, half:]).astype(BF16).astype(F32)
            spread(q_rope, n, jnp.concatenate([q_r, jnp.zeros((tok, LANES - rope_dim), F32)], axis=1))
    lat_back.start()
    rope_back.start()

    rows, keys = GROUP * n_heads, GROUP * seq
    key = lax.broadcasted_iota(jnp.int32, (rows, keys), 1)
    same = (key // seq) == (lax.broadcasted_iota(jnp.int32, (rows, keys), 0) // n_heads)
    key_tok, key_seq = key // seq, lax.rem(key, seq)
    across = (((1,), (1,)), ((), ()))
    for g in range(tok // GROUP):
        lat_g = lat[g * GROUP:(g + 1) * GROUP].reshape(keys, rank)
        rope_g = rope[g * GROUP:(g + 1) * GROUP].reshape(keys, rope_dim)
        sl = slice(g * rows, (g + 1) * rows)
        scores = lax.dot_general(jnp.concatenate([q_lat[c, sl] for c in range(rank // LANES)], axis=1).astype(BF16), lat_g, across, preferred_element_type=F32)
        scores = scores + lax.dot_general(q_rope[0, sl, :rope_dim].astype(BF16), rope_g, across, preferred_element_type=F32)
        scores = scores * head ** -0.5
        last = jnp.full((rows, keys), pos_ref[g * GROUP], jnp.int32)
        for i in range(1, GROUP):
            last = jnp.where(key_tok == i, pos_ref[g * GROUP + i], last)
        scores = jnp.where(same & (key_seq <= last), scores, -jnp.inf)
        top = jnp.max(scores, axis=1, keepdims=True)
        expd = jnp.exp(scores - top)
        probs = (expd / jnp.sum(expd, axis=1, keepdims=True)).astype(BF16)
        o_g = dot32(probs, lat_g).astype(BF16).astype(F32)
        for c in range(rank // LANES):
            o_lat[c, sl] = o_g[:, c * LANES:(c + 1) * LANES]

    uv_copy.wait()
    for n in range(n_heads):
        o_n = jnp.concatenate([o_lat[c, pl.ds(n, tok, stride=n_heads), :] for c in range(rank // LANES)], axis=1).astype(BF16)
        o_heads[:, n * uv.shape[2]:(n + 1) * uv.shape[2]] = dot32(o_n, uv[n]).astype(BF16)
    wr_copy.wait()
    wo_copy.wait()
    for start, width in wide_tiles(dim, 512):
        attn = dot32(o_heads[...], wo[:, start:start + width])
        res_ref[:, start:start + width] = (x[:, start:start + width] + attn).astype(BF16)
    h = (unit_norm(res_ref[...].astype(F32)) * fg_ref[...].astype(F32)).astype(BF16)
    h_ref[...] = h

    gate = jax.nn.sigmoid(dot32(h, wr[...]))
    ids = ids_ref[...]
    exp_lane = lax.broadcasted_iota(jnp.int32, (tok, n_exp), 1)
    listed = jnp.zeros((tok, n_exp), F32)
    for i in range(ids_ref.shape[1]):
        listed = listed + jnp.where(exp_lane == ids[:, i:i + 1], 1.0, 0.0)
    lower = lax.broadcasted_iota(jnp.int32, (tok, tok), 0) >= lax.broadcasted_iota(jnp.int32, (tok, tok), 1)
    slots = dot32(jnp.where(lower, 1.0, 0.0).astype(BF16), listed.astype(BF16)) * listed
    chosen = gate * listed
    table_ref[:, :n_exp] = ROUTE_SCALE * chosen / jnp.sum(chosen, axis=1, keepdims=True)
    table_ref[:, n_exp:] = slots
    lat_back.wait()
    rope_back.wait()


def attn_call(tok_in, lat_cache, rope_cache, tok_pos, expert_ids, attn_gain, w_query, w_kvdown, w_ukey, w_uval, w_out, ffn_gain, w_router):
    tok, dim = tok_in.shape
    n_heads, nope, rank = w_ukey.shape
    seq, rope_dim = rope_cache.shape[1:]
    n_exp = w_router.shape[1]
    blocks = n_heads // GROUP
    inv_freq = ROPE_BASE ** (-(2.0 * jnp.arange(rope_dim // 2)) / rope_dim)
    angle = tok_pos.astype(F32)[:, None] * inv_freq[None, :]
    trig = jnp.concatenate([jnp.cos(angle), jnp.sin(angle)], axis=1)
    vmem = pl.BlockSpec(memory_space=pltpu.VMEM)
    hbm = pl.BlockSpec(memory_space=pl.ANY)
    dma = pltpu.SemaphoreType.DMA
    return pl.pallas_call(
        attn_kernel,
        out_shape=[
            jax.ShapeDtypeStruct((tok, dim), BF16),
            jax.ShapeDtypeStruct((tok, dim), BF16),
            jax.ShapeDtypeStruct((tok, 2 * n_exp), F32),
            jax.ShapeDtypeStruct(lat_cache.shape, BF16),
            jax.ShapeDtypeStruct(rope_cache.shape, BF16),
        ],
        in_specs=[pl.BlockSpec(memory_space=pltpu.SMEM)] + [vmem] * 5 + [hbm] * 8,
        out_specs=[vmem, vmem, vmem, hbm, hbm],
        scratch_shapes=[
            pltpu.VMEM((blocks, dim, w_query.shape[1] // blocks), BF16),
            pltpu.VMEM(w_kvdown.shape, BF16),
            pltpu.VMEM(w_ukey.shape, BF16),
            pltpu.VMEM(w_uval.shape, BF16),
            pltpu.VMEM(w_out.shape, BF16),
            pltpu.VMEM(w_router.shape, BF16),
            pltpu.VMEM(lat_cache.shape, BF16),
            pltpu.VMEM(rope_cache.shape, BF16),
            pltpu.VMEM((rank // LANES, tok * n_heads, LANES), F32),
            pltpu.VMEM((1, tok * n_heads, LANES), F32),
            pltpu.VMEM((rank // LANES, tok * n_heads, LANES), F32),
            pltpu.VMEM((tok, w_out.shape[0]), BF16),
            dma((blocks,)), dma((5,)), dma((2,)), dma((2,)),
        ],
        compiler_params=pltpu.CompilerParams(vmem_limit_bytes=60000000),
        name='latent_attention',
    )(tok_pos, tok_in, trig, expert_ids, attn_gain[None, :], ffn_gain[None, :], w_query, w_kvdown, w_ukey, w_uval, w_out, w_router, lat_cache, rope_cache)


def moe_kernel(n_ep, n_exp, h_ref, table_ref, resid_ref, rowpat_ref, colpat_ref,
               sg_ref, su_ref, sd_ref, eg_ref, eu_ref, ed_ref, out_ref,
               hall, gall, xg, act, act_sh, ebuf, esib, cmat, ct, ring, wa, wb, sh_out,
               sem_a, sem_b, ag_send, ag_recv, sib_send, sib_recv, tb_send, tb_recv, ts_send, ts_recv,
               ex_send, ex_recv, rg_send, rg_recv):
    nz = n_ep // 2
    far = nz // 2
    tok, dim = h_ref.shape
    e_loc, _, ff = eg_ref.shape
    halves = sg_ref.shape[1] // ff
    rows_par = nz * CAP
    rows_exp = 2 * rows_par
    rows_all = e_loc * rows_exp
    rows_q = e_loc * rows_par
    cw = dim // CHUNKS
    half_dim = dim // 2

    me = lax.axis_index('ep')
    z = me // 2
    par = lax.rem(me, 2)
    sib = me + 1 - 2 * par
    up_dev = lax.rem(z + 1, nz) * 2 + par
    dn_dev = lax.rem(z + nz - 1, nz) * 2 + par

    def chip(step):
        return lax.rem(z + step + 2 * nz, nz)

    def slot_of(p, zz):
        return p * nz + zz

    def a_slot(unit):
        return unit % SLOTS_A if unit < 2 * e_loc else unit - 2 * e_loc

    def a_copy(unit):
        slot = a_slot(unit)
        if unit < 2 * e_loc:
            src = (eg_ref if unit % 2 == 0 else eu_ref).at[unit // 2]
        else:
            hf = (unit - 2 * e_loc) // 2
            src = (sg_ref if unit % 2 == 0 else su_ref).at[:, pl.ds(hf * ff, ff)]
        return pltpu.make_async_copy(src, wa.at[slot], sem_a.at[unit])

    def b_place(unit):
        if unit >= CHUNKS * e_loc + SLOTS_B:
            pos = unit - CHUNKS * e_loc - SLOTS_B
            slot, side = 5 + pos // 2, pos % 2
        elif unit >= CHUNKS * e_loc:
            return wb.at[unit - CHUNKS * e_loc]
        elif unit >= SLOTS_B:
            slot, side = 1 + (unit - SLOTS_B) // 2, unit % 2
        else:
            return wb.at[unit]
        return wa.at[slot, pl.ds(0, ff), pl.ds(side * cw, cw)]

    def b_copy(unit):
        if unit < CHUNKS * e_loc:
            j, e = unit // e_loc, unit % e_loc
            src = ed_ref.at[e, :, pl.ds(j * cw, cw)]
        else:
            j, hf = (unit - CHUNKS * e_loc) // halves, (unit - CHUNKS * e_loc) % halves
            src = sd_ref.at[pl.ds(hf * ff, ff), pl.ds(j * cw, cw)]
        return pltpu.make_async_copy(src, b_place(unit), sem_b.at[unit])

    for unit in range(SLOTS_A):
        a_copy(unit).start()
    for unit in range(SLOTS_B):
        b_copy(unit).start()

    barrier = pltpu.get_barrier_semaphore()
    for dev in (up_dev, dn_dev, sib):
        pl.semaphore_signal(barrier, inc=1, device_id={'ep': dev}, device_id_type=MESH)
    pl.semaphore_wait(barrier, 3)

    def remote(src, dst, send, recv, dev):
        return pltpu.make_async_remote_copy(src_ref=src, dst_ref=dst, send_sem=send, recv_sem=recv,
                                            device_id={'ep': dev}, device_id_type=MESH)

    def h_hop(way, step, half):
        dev = up_dev if way == 0 else dn_dev
        origin = chip(-step if way == 0 else step)
        slot = slot_of(par, origin)
        cols = pl.ds(half * half_dim, half_dim)
        src = h_ref.at[:, cols] if step == 0 else hall.at[slot, :, cols]
        return remote(src, hall.at[slot, :, cols], ag_send.at[way, step, half], ag_recv.at[way, step, half], dev)

    def t_hop(way, step):
        dev = up_dev if way == 0 else dn_dev
        origin = chip(-step if way == 0 else step)
        slot = slot_of(par, origin)
        src = table_ref if step == 0 else gall.at[slot]
        return remote(src, gall.at[slot], tb_send.at[way, step], tb_recv.at[way, step], dev)

    def h_cross(k, origin):
        slot = slot_of(par, origin)
        src = h_ref if k == 0 else hall.at[slot]
        return remote(src, hall.at[slot], sib_send.at[k], sib_recv.at[k], sib)

    def t_cross(k, origin):
        slot = slot_of(par, origin)
        src = table_ref if k == 0 else gall.at[slot]
        return remote(src, gall.at[slot], ts_send.at[k], ts_recv.at[k], sib)

    t_steps = (far, far - 1)
    sent = []

    def go(copy):
        copy.start()
        sent.append(copy)
        return copy

    hops, thops = {}, {}
    for way in range(2):
        thops[way, 0] = go(t_hop(way, 0))
    for half in range(2):
        for way in range(2):
            hops[way, 0, half] = go(h_hop(way, 0, half))
    crossed = [go(t_cross(0, z)), go(h_cross(0, z))]
    hall[slot_of(par, z)] = h_ref[...]
    gall[slot_of(par, z)] = table_ref[...]
    for step in range(far):
        for way in range(2):
            if step < t_steps[way]:
                origin = chip(-(step + 1) if way == 0 else step + 1)
                thops[way, step].wait_recv()
                if step + 1 < t_steps[way]:
                    thops[way, step + 1] = go(t_hop(way, step + 1))
                crossed.append(go(t_cross(1 + 2 * step + way, origin)))
        for half in range(2):
            for way in range(2):
                if step < far - 1 or half == way:
                    hops[way, step, half].wait_recv()
                if step < far - 2 or (step == far - 2 and half == way):
                    hops[way, step + 1, half] = go(h_hop(way, step + 1, half))
        if step < far - 1:
            for way in range(2):
                crossed.append(go(h_cross(1 + 2 * step + way, chip(-(step + 1) if way == 0 else step + 1))))
    crossed.append(go(h_cross(2 * far - 1, chip(far))))
    for copy in crossed:
        copy.wait_recv()

    rowpat = rowpat_ref[...]
    row_exp, row_dev, row_slot = rowpat[:, 0:1], rowpat[:, 1:2], rowpat[:, 2:3]
    base = n_exp + e_loc * me
    lane = lax.broadcasted_iota(jnp.int32, (rows_all, LANES), 1)
    pick = jnp.where(lane == base + row_exp.astype(jnp.int32), 1.0, 0.0).astype(BF16)
    slots_by_row = lax.dot_general(pick, gall[...].reshape(n_ep * tok, LANES).astype(BF16), (((1,), (1,)), ((), ())),
                                   preferred_element_type=F32)
    tok_dev = (lax.broadcasted_iota(jnp.int32, (rows_all, n_ep * tok), 1) // tok).astype(F32)
    place = jnp.where((slots_by_row == row_slot) & (tok_dev == row_dev), 1.0, 0.0).astype(BF16)
    for start, width in wide_tiles(dim, 256):
        rows = hall[:, :, start:start + width].reshape(n_ep * tok, width)
        xg[:, :, start:start + width] = dot32(place, rows).astype(BF16).reshape(e_loc, rows_exp, width)

    colpat = colpat_ref[...]
    col_exp, col_chip, col_slot = colpat[0:1, :], colpat[1:2, :], colpat[2:3, :]
    g_own = gall[pl.ds(par * nz, nz)].reshape(nz * tok, LANES)
    part1 = g_own.astype(BF16)
    rest1 = g_own - part1.astype(F32)
    part2 = rest1.astype(BF16)
    part3 = (rest1 - part2.astype(F32)).astype(BF16)
    sub = lax.broadcasted_iota(jnp.int32, (LANES, rows_q), 0)
    tok_chip = (lax.broadcasted_iota(jnp.int32, (nz * tok, rows_q), 0) // tok).astype(F32)
    for q in range(2):
        ids = e_loc * (me if q == 0 else sib) + col_exp.astype(jnp.int32)
        sel_w = jnp.where(sub == ids, 1.0, 0.0).astype(BF16)
        sel_s = jnp.where(sub == n_exp + ids, 1.0, 0.0).astype(BF16)
        here = (dot32(part1, sel_s) == col_slot) & (tok_chip == col_chip)
        for i, part in enumerate((part1, part2, part3)):
            cmat[q, i] = jnp.where(here, dot32(part, sel_w), 0.0).astype(BF16)

    def swiglu_tile(x, slot_g, slot_u, start, width):
        gate = dot32(x, wa[slot_g, :, start:start + width])
        up = dot32(x, wa[slot_u, :, start:start + width])
        return (jax.nn.silu(gate) * up).astype(BF16)

    def expert_up(e, carry):
        slot_g = lax.rem(2 * e, SLOTS_A)
        slot_u = lax.rem(2 * e + 1, SLOTS_A)
        for unit, slot in ((2 * e, slot_g), (2 * e + 1, slot_u)):
            pltpu.make_async_copy(eg_ref.at[0], wa.at[slot], sem_a.at[unit]).wait()
        for start, width in wide_tiles(ff, 256):
            act[e, :, start:start + width] = swiglu_tile(xg[e], slot_g, slot_u, start, width)
        for e_st in range(e_loc):
            @pl.when(e == e_st)
            def _():
                if e_st == 0:
                    a_copy(SLOTS_A).start()
                    ahead = (4, 5)
                elif e_st < e_loc - 1:
                    ahead = range(4 * e_st + 2, 4 * e_st + 6)
                else:
                    ahead = (14, 15)
                for unit in ahead:
                    b_copy(unit).start()
                if e_st == e_loc - 1:
                    a_copy(2 * e_loc).start()
        return carry

    lax.fori_loop(0, e_loc, expert_up, 0)

    def reach(way, j):
        return far if (way + j) % 2 == 0 else nz - 1 - far

    def ring_copy(way, j, step):
        dev = up_dev if way == 0 else dn_dev
        ahead = reach(way, j) - step + 1
        dest = chip(ahead if way == 0 else -ahead)
        src = ct.at[j, dest] if step == 1 else ring.at[way, j, step - 2]
        return remote(src, ring.at[way, j, step - 1], rg_send.at[way, j, step - 1], rg_recv.at[way, j, step - 1], dev)

    rcopies = {}

    def combine(j):
        exch[j].wait_recv()
        own = ebuf[j, par].reshape(rows_q, cw)
        other = esib[j].reshape(rows_q, cw)
        for start, width in wide_tiles(cw, 256):
            total = dot32(cmat[0, 0], own[:, start:start + width]) + dot32(cmat[1, 0], other[:, start:start + width])
            for i in (1, 2):
                total += dot32(cmat[0, i], own[:, start:start + width]) + dot32(cmat[1, i], other[:, start:start + width])
            ct[j, :, :, start:start + width] = total.reshape(nz, tok, width)
        for way in range(2):
            rcopies[way, j, 1] = go(ring_copy(way, j, 1))

    def advance(j, step):
        for way in range(2):
            if step < reach(way, j):
                rcopies[way, j, step].wait_recv()
                ahead = reach(way, j) - step
                dest = chip(ahead if way == 0 else -ahead)
                ring[way, j, step - 1] += ct[j, dest]
                rcopies[way, j, step + 1] = go(ring_copy(way, j, step + 1))

    def finish(j):
        cols = slice(j * cw, (j + 1) * cw)
        total = resid_ref[:, cols].astype(F32) + sh_out[:, cols] + ct[j, z]
        for way in range(2):
            rcopies[way, j, reach(way, j)].wait_recv()
            total += ring[way, j, reach(way, j) - 1]
        out_ref[:, cols] = total.astype(BF16)

    exch = {}

    def down(j):
        for e in range(e_loc):
            b_copy(j * e_loc + e).wait()
        for e in range(e_loc):
            res = dot32(act[e], b_place(j * e_loc + e)[...]).astype(BF16)
            ebuf[j, 0, e] = res[:rows_par]
            ebuf[j, 1, e] = res[rows_par:]
        exch[j] = go(remote(ebuf.at[j, 1 - par], esib.at[j], ex_send.at[j], ex_recv.at[j], sib))
        shared = CHUNKS * e_loc
        if j == 1:
            a_copy(2 * e_loc + 1).start()
            a_copy(2 * e_loc + 2).start()
        elif j == 2:
            a_copy(2 * e_loc + 3).start()
            for pos in range(SLOTS_B):
                b_copy(shared + pos).start()
        elif j == 3:
            for pos in range(SLOTS_B, CHUNKS * halves):
                b_copy(shared + pos).start()

    def shared_up(hf, tile):
        unit = 2 * e_loc + 2 * hf
        start, width = wide_tiles(ff, 256)[tile]
        if tile == 0:
            a_copy(unit).wait()
            a_copy(unit + 1).wait()
        act_sh[hf, :, start:start + width] = swiglu_tile(h_ref[...], a_slot(unit), a_slot(unit + 1), start, width)

    def shared_down(j):
        total = jnp.zeros((tok, cw), F32)
        for hf in range(halves):
            unit = CHUNKS * e_loc + j * halves + hf
            b_copy(unit).wait()
            total += dot32(act_sh[hf], b_place(unit)[...])
        sh_out[:, j * cw:(j + 1) * cw] = total

    down(0)
    down(1)
    combine(0)
    down(2)
    combine(1)
    advance(0, 1)
    down(3)
    combine(2)
    advance(1, 1)
    advance(0, 2)
    combine(3)
    tiles = len(wide_tiles(ff, 256))
    pieces = [functools.partial(shared_up, hf, tile) for hf in range(halves) for tile in range(tiles)]
    pieces += [functools.partial(shared_down, j) for j in range(CHUNKS)]
    events = [(2, 1), (1, 2), (3, 1), (0, 3), (2, 2), (1, 3), (3, 2), (2, 3), (3, 3)]
    for i, event in enumerate(events):
        advance(*event)
        for piece in pieces[i * len(pieces) // len(events):(i + 1) * len(pieces) // len(events)]:
            piece()
    for j in range(CHUNKS):
        finish(j)
    for copy in sent:
        copy.wait_send()


def moe_call(n_ep, h_norm, table, resid, w_sg, w_su, w_sd, w_eg, w_eu, w_ed):
    nz = n_ep // 2
    tok, dim = h_norm.shape
    e_loc, _, ff = w_eg.shape
    n_exp = e_loc * n_ep
    halves = w_sg.shape[1] // ff
    far = nz // 2
    cw = dim // CHUNKS
    rows_par = nz * CAP
    rows_exp = 2 * rows_par
    rows_all = e_loc * rows_exp
    rows_q = e_loc * rows_par
    row = np.arange(rows_all)
    rowpat = np.zeros((rows_all, 8), np.float32)
    rowpat[:, 0] = row // rows_exp
    rowpat[:, 1] = (row % rows_exp) // CAP
    rowpat[:, 2] = row % CAP + 1
    col = np.arange(rows_q)
    colpat = np.zeros((8, rows_q), np.float32)
    colpat[0] = col // rows_par
    colpat[1] = (col % rows_par) // CAP
    colpat[2] = col % CAP + 1
    vmem = pl.BlockSpec(memory_space=pltpu.VMEM)
    hbm = pl.BlockSpec(memory_space=pl.ANY)
    dma = pltpu.SemaphoreType.DMA
    return pl.pallas_call(
        functools.partial(moe_kernel, n_ep, n_exp),
        out_shape=jax.ShapeDtypeStruct((tok, dim), BF16),
        in_specs=[vmem] * 5 + [hbm] * 6,
        out_specs=vmem,
        scratch_shapes=[
            pltpu.VMEM((n_ep, tok, dim), BF16),
            pltpu.VMEM((n_ep, tok, LANES), F32),
            pltpu.VMEM((e_loc, rows_exp, dim), BF16),
            pltpu.VMEM((e_loc, rows_exp, ff), BF16),
            pltpu.VMEM((halves, tok, ff), BF16),
            pltpu.VMEM((CHUNKS, 2, e_loc, rows_par, cw), BF16),
            pltpu.VMEM((CHUNKS, e_loc, rows_par, cw), BF16),
            pltpu.VMEM((2, 3, nz * tok, rows_q), BF16),
            pltpu.VMEM((CHUNKS, nz, tok, cw), F32),
            pltpu.VMEM((2, CHUNKS, far, tok, cw), F32),
            pltpu.VMEM((SLOTS_A, dim, ff), BF16),
            pltpu.VMEM((SLOTS_B, ff, cw), BF16),
            pltpu.VMEM((tok, dim), F32),
            dma((2 * (e_loc + halves),)), dma((CHUNKS * (e_loc + halves),)),
            dma((2, far, 2)), dma((2, far, 2)), dma((nz,)), dma((nz,)),
            dma((2, far)), dma((2, far)), dma((nz,)), dma((nz,)),
            dma((CHUNKS,)), dma((CHUNKS,)),
            dma((2, CHUNKS, far)), dma((2, CHUNKS, far)),
        ],
        compiler_params=pltpu.CompilerParams(collective_id=0, has_side_effects=True, vmem_limit_bytes=67000000),
        name='moe_ring',
    )(h_norm, table, resid, jnp.asarray(rowpat), jnp.asarray(colpat), w_sg, w_su, w_sd, w_eg, w_eu, w_ed)


def solution(mesh):
    n_ep = mesh.shape['ep']
    row_one = P(('dp', 'ep'))
    row_two = P(('dp', 'ep'), None)
    row_three = P(('dp', 'ep'), None, None)
    rep_one = P(None)
    rep_two = P(None, None)
    rep_three = P(None, None, None)
    exp_spec = P('ep', None, None)

    def local_step(tok_in, lat_cache, rope_cache, tok_pos, expert_ids, attn_gain, w_query, w_kvdown, w_ukey, w_uval, w_out, ffn_gain, w_router, sh_gate, sh_up, sh_down, ex_gate, ex_up, ex_down):
        resid_bf, h_norm, table, lat_out, rope_out = attn_call(tok_in, lat_cache, rope_cache, tok_pos, expert_ids, attn_gain, w_query, w_kvdown, w_ukey, w_uval, w_out, ffn_gain, w_router)
        out_hidden = moe_call(n_ep, h_norm, table, resid_bf, sh_gate, sh_up, sh_down, ex_gate, ex_up, ex_down)
        return out_hidden, lat_out, rope_out

    in_specs = (row_two, row_three, row_three, row_one, row_two, rep_one, rep_two, rep_two, rep_three, rep_three, rep_two, rep_one, rep_two, rep_two, rep_two, rep_two, exp_spec, exp_spec, exp_spec)
    out_specs = (row_two, row_three, row_three)
    return jax.shard_map(local_step, mesh=mesh, in_specs=in_specs, out_specs=out_specs, check_vma=False)
```

time: 104 us -> 99.9 us (0.961)
  the two profiles are of different devices: /device:TPU:21 before, /device:TPU:30 now
where the time goes in v2:
time: 99.9 us; the launch traced here: 99.6 us
  Pallas kernels  85.7 us (86%)
  local copies, waits for them, and re-layouts  11.8 us (12%)
  other arithmetic  1.49 us (1%)
    pallas_call x1, Pallas kernels, moe_call(): pl.pallas_call(functools.partial(moe_kernel, n_ep, n_exp), out_shape=jax....  66.2 us
    pallas_call x1, Pallas kernels, attn_call(): pl.pallas_call(attn_kernel, out_shape=[jax.ShapeDtypeStruct((tok, dim), B...  19.4 us
    unnamed x4, local copies, waits for them, and re-layouts  9.22 us

profile of v2, /device:TPU:30, one launch (start us, length us, event | category | flops | bytes accessed | tf_op | source)
XLA Modules:
  0.0 99.6 jit_solution(2521208342071104851)
XLA Ops:
  0.6 0.7 convert_element_type.10
  1.3 1.3 %broadcast_in_dim.8.ag_ref = bf16[1,2048]{1,0:T(2,128)(2,1)} reshape(bf16[2048]{0:T(1024)(128)(2,1)} %param.26) | data formatting | bytes 8192 | tf_op jit(solution)/shard_map/broadcast_in_dim | solution.py:200
  2.6 1.3 %broadcast_in_dim.9.fg_ref = bf16[1,2048]{1,0:T(2,128)(2,1)} reshape(bf16[2048]{0:T(1024)(128)(2,1)} %param.32) | data formatting | bytes 8192 | tf_op jit(solution)/shard_map/broadcast_in_dim | solution.py:200
  3.9 1.4 %copy.24.ids_ref = s32[32,6]{1,0:T(8,128)} copy(s32[32,6]{0,1:T(8,128)} %param.25) | data formatting | bytes 1536 | tf_op args[4]
  5.2 0.1 multiply_cosine_fusion
  5.4 0.7 pad_maximum_fusion.trig_ref
  6.1 2.0 %copy.26.wr_ref = bf16[2048,64]{1,0:T(8,128)(2,1)} copy(bf16[2048,64]{0,1:T(8,128)(2,1)} %param.33) | data formatting | bytes 524288 | tf_op args[12]
  8.0 4.3 %copy.25.wkv_ref = bf16[2048,576]{1,0:T(8,128)(2,1)} copy(bf16[2048,576]{0,1:T(8,128)(2,1)} %param.28) | data formatting | bytes 4718592 | tf_op args[7]
  12.4 19.4 %latent_attention.1 = (bf16[32,2048]{1,0:T(8,128)(2,1)}, bf16[32,2048]{1,0:T(8,128)(2,1)}, f32[32,128]{1,0:T(8,128)}, bf16[32,64,512]{2,1,0:T(8,128)(2,1)}, bf16[32,64,64]{2,1,0:T(8,128)(2,1)}) custom-call(s32[32]{0:T(128)} %pos_ref.1, bf16[32,2048]{1,0:T(8,128)(2,1)} %x_ref.1, f32[32,64]{1,0:T(8,128)} %pad_maximum_fusion.trig_ref, s32[32,6]{1,0:T(8,128)} %copy.24.ids_ref, ...), custom_call_target="tpu_custom_call" | custom-call | tf_op jit(solution)/shard_map/latent_attention/pallas_call | solution.py:172
  31.8 66.2 %moe_ring.1 = bf16[32,2048]{1,0:T(8,128)(2,1)} custom-call(bf16[32,2048]{1,0:T(8,128)(2,1)} %get-tuple-element.8.h_ref, f32[32,128]{1,0:T(8,128)} %get-tuple-element.9.table_ref, bf16[32,2048]{1,0:T(8,128)(2,1)} %get-tuple-element.10.resid_ref, f32[384,8]{1,0:T(8,128)} %constant.11.clone.rowpat_ref, f32[8,192]{1,0:T(8,128)} %constant.12.clone.colpat_ref, ...), custom_call_target="tpu_custom_call" | custom-call | tf_op jit(solution)/shard_map/moe_ring/pallas_call | solution.py:532
  98.0 1.6 %copy.28 = bf16[32,2048]{1,0:T(8,128)(2,1)} copy(bf16[32,2048]{1,0:T(8,128)(2,1)} %moe_ring.1) | data formatting | bytes 262144
  (1 shorter events, 0.0 us)

commit v3 on v2

--- a/solution.py
+++ b/solution.py
@@ -18,6 +18,7 @@
 SLOTS_A = 7
 SLOTS_B = 4
 CAP = 6
+PARTS = 4
 LANES = 128
 GROUP = 4
 
@@ -35,15 +36,15 @@
     return [(start, min(width, total - start)) for start in range(0, total, width)]
 
 
-def attn_kernel(pos_ref, x_ref, trig_ref, ids_ref, ag_ref, fg_ref, wq_ref, wkv_ref, uk_ref, uv_ref, wo_ref, wr_ref, lat_ref, rope_ref,
+def attn_kernel(pos_ref, x_ref, freq_ref, ids_ref, ag_ref, fg_ref, wq_ref, wkv_ref, uk_ref, uv_ref, wo_ref, wr_ref, lat_ref, rope_ref,
                 res_ref, h_ref, table_ref, lat_out, rope_out,
-                wq, wkv, uk, uv, wo, wr, lat, rope, q_lat, q_rope, o_lat, o_heads, sem_q, sem_w, sem_c, sem_o):
+                wq, wkv, uk, uv, wo, wr, lat, rope, q_lat, q_rope, o_lat, o_heads, score, prob, sem_q, sem_w, sem_c, sem_o):
     n_heads, nope, rank = uk_ref.shape
     tok, dim = x_ref.shape
     seq, rope_dim = rope_ref.shape[1:]
     half = rope_dim // 2
     head = nope + rope_dim
-    n_exp = wr_ref.shape[1]
+    n_exp = wr_ref.shape[0]
     blocks = n_heads // GROUP
     q_cols = GROUP * head
 
@@ -58,35 +59,29 @@
     lat_copy = pltpu.make_async_copy(lat_ref, lat, sem_c.at[0])
     rope_copy = pltpu.make_async_copy(rope_ref, rope, sem_c.at[1])
     kv_copy.start()
-    lat_copy.start()
-    rope_copy.start()
+    q_copy(0).start()
     uk_copy.start()
-    for blk in range(blocks):
-        q_copy(blk).start()
-    uv_copy.start()
-    wr_copy.start()
-    wo_copy.start()
 
     x = x_ref[...].astype(F32)
-    x_norm = (unit_norm(x) * ag_ref[...].astype(F32)).astype(BF16)
-    cos, sin = trig_ref[:, :half], trig_ref[:, half:]
+    x_norm = (unit_norm(x) * ag_ref[...].astype(F32).reshape(1, dim)).astype(BF16)
+    tok_row = lax.broadcasted_iota(jnp.int32, (tok, half), 0)
+    pos = jnp.zeros((tok, half), jnp.int32)
+    for t in range(tok):
+        pos = jnp.where(tok_row == t, pos_ref[t], pos)
+    angle = pos.astype(F32) * freq_ref[...]
+    cos, sin = jnp.cos(angle), jnp.sin(angle)
+    across = (((1,), (1,)), ((), ()))
 
     def rotate(first, second):
         return jnp.concatenate([first * cos - second * sin, second * cos + first * sin], axis=1)
 
     kv_copy.wait()
-    kv = dot32(x_norm, wkv[...])
+    q_copy(1).start()
+    if blocks > 2:
+        q_copy(2).start()
+    kv = lax.dot_general(x_norm, wkv[...], across, preferred_element_type=F32)
     lat_new = unit_norm(kv[:, :rank]).astype(BF16).astype(F32)
     rope_new = rotate(kv[:, rank:rank + half], kv[:, rank + half:]).astype(BF16).astype(F32)
-    lat_copy.wait()
-    rope_copy.wait()
-    for t in range(tok):
-        here = lax.broadcasted_iota(jnp.int32, (seq, rank), 0) == pos_ref[t]
-        lat[t] = jnp.where(here, lat_new[t:t + 1], lat[t].astype(F32)).astype(BF16)
-        here = lax.broadcasted_iota(jnp.int32, (seq, rope_dim), 0) == pos_ref[t]
-        rope[t] = jnp.where(here, rope_new[t:t + 1], rope[t].astype(F32)).astype(BF16)
-    lat_back = pltpu.make_async_copy(lat, lat_out, sem_o.at[0])
-    rope_back = pltpu.make_async_copy(rope, rope_out, sem_o.at[1])
 
     def spread(ref, n, val):
         for c in range(val.shape[1] // LANES):
@@ -95,6 +90,16 @@
     uk_copy.wait()
     for blk in range(blocks):
         q_copy(blk).wait()
+        if blk == 0:
+            lat_copy.start()
+            rope_copy.start()
+            if blocks > 3:
+                q_copy(3).start()
+        elif blk == 1:
+            uv_copy.start()
+            wr_copy.start()
+        if blk == blocks - 2:
+            wo_copy.start()
         q = dot32(x_norm, wq[blk]).astype(BF16)
         for i in range(GROUP):
             n = blk * GROUP + i
@@ -104,31 +109,45 @@
             q_r = q[:, at + nope:at + head].astype(F32)
             q_r = rotate(q_r[:, :half], q_r[:, half:]).astype(BF16).astype(F32)
             spread(q_rope, n, jnp.concatenate([q_r, jnp.zeros((tok, LANES - rope_dim), F32)], axis=1))
-    lat_back.start()
-    rope_back.start()
-
+    lat_copy.wait()
+    rope_copy.wait()
     rows, keys = GROUP * n_heads, GROUP * seq
     key = lax.broadcasted_iota(jnp.int32, (rows, keys), 1)
     same = (key // seq) == (lax.broadcasted_iota(jnp.int32, (rows, keys), 0) // n_heads)
     key_tok, key_seq = key // seq, lax.rem(key, seq)
-    across = (((1,), (1,)), ((), ()))
-    for g in range(tok // GROUP):
+    groups = tok // GROUP
+
+    def grouped(g):
         lat_g = lat[g * GROUP:(g + 1) * GROUP].reshape(keys, rank)
         rope_g = rope[g * GROUP:(g + 1) * GROUP].reshape(keys, rope_dim)
-        sl = slice(g * rows, (g + 1) * rows)
-        scores = lax.dot_general(jnp.concatenate([q_lat[c, sl] for c in range(rank // LANES)], axis=1).astype(BF16), lat_g, across, preferred_element_type=F32)
-        scores = scores + lax.dot_general(q_rope[0, sl, :rope_dim].astype(BF16), rope_g, across, preferred_element_type=F32)
-        scores = scores * head ** -0.5
+        return slice(g * rows, (g + 1) * rows), lat_g, rope_g
+
+    lat_row = lax.broadcasted_iota(jnp.int32, (seq, rank), 0)
+    rope_row = lax.broadcasted_iota(jnp.int32, (seq, rope_dim), 0)
+    for t in range(tok):
+        lat[t] = jnp.where(lat_row == pos_ref[t], lat_new[t:t + 1], lat[t].astype(F32)).astype(BF16)
+        rope[t] = jnp.where(rope_row == pos_ref[t], rope_new[t:t + 1], rope[t].astype(F32)).astype(BF16)
+    lat_back = pltpu.make_async_copy(lat, lat_out, sem_o.at[0])
+    rope_back = pltpu.make_async_copy(rope, rope_out, sem_o.at[1])
+    for g in range(groups):
+        sl, lat_g, rope_g = grouped(g)
+        q_g = jnp.concatenate([q_lat[c, sl] for c in range(rank // LANES)], axis=1).astype(BF16)
+        score[g] = (lax.dot_general(q_g, lat_g, across, preferred_element_type=F32)
+                    + lax.dot_general(q_rope[0, sl, :rope_dim].astype(BF16), rope_g, across, preferred_element_type=F32))
+    for g in range(groups):
         last = jnp.full((rows, keys), pos_ref[g * GROUP], jnp.int32)
         for i in range(1, GROUP):
             last = jnp.where(key_tok == i, pos_ref[g * GROUP + i], last)
-        scores = jnp.where(same & (key_seq <= last), scores, -jnp.inf)
-        top = jnp.max(scores, axis=1, keepdims=True)
-        expd = jnp.exp(scores - top)
-        probs = (expd / jnp.sum(expd, axis=1, keepdims=True)).astype(BF16)
-        o_g = dot32(probs, lat_g).astype(BF16).astype(F32)
+        masked = jnp.where(same & (key_seq <= last), score[g] * head ** -0.5, -jnp.inf)
+        expd = jnp.exp(masked - jnp.max(masked, axis=1, keepdims=True))
+        prob[g] = (expd / jnp.sum(expd, axis=1, keepdims=True)).astype(BF16)
+    for g in range(groups):
+        sl, lat_g, _ = grouped(g)
+        o_g = dot32(prob[g], lat_g).astype(BF16).astype(F32)
         for c in range(rank // LANES):
             o_lat[c, sl] = o_g[:, c * LANES:(c + 1) * LANES]
+    lat_back.start()
+    rope_back.start()
 
     uv_copy.wait()
     for n in range(n_heads):
@@ -139,17 +158,18 @@
     for start, width in wide_tiles(dim, 512):
         attn = dot32(o_heads[...], wo[:, start:start + width])
         res_ref[:, start:start + width] = (x[:, start:start + width] + attn).astype(BF16)
-    h = (unit_norm(res_ref[...].astype(F32)) * fg_ref[...].astype(F32)).astype(BF16)
+    h = (unit_norm(res_ref[...].astype(F32)) * fg_ref[...].astype(F32).reshape(1, dim)).astype(BF16)
     h_ref[...] = h
 
-    gate = jax.nn.sigmoid(dot32(h, wr[...]))
-    ids = ids_ref[...]
-    exp_lane = lax.broadcasted_iota(jnp.int32, (tok, n_exp), 1)
-    listed = jnp.zeros((tok, n_exp), F32)
-    for i in range(ids_ref.shape[1]):
-        listed = listed + jnp.where(exp_lane == ids[:, i:i + 1], 1.0, 0.0)
-    lower = lax.broadcasted_iota(jnp.int32, (tok, tok), 0) >= lax.broadcasted_iota(jnp.int32, (tok, tok), 1)
-    slots = dot32(jnp.where(lower, 1.0, 0.0).astype(BF16), listed.astype(BF16)) * listed
+    gate = jax.nn.sigmoid(lax.dot_general(h, wr[...], across, preferred_element_type=F32))
+    exp_row = lax.broadcasted_iota(jnp.int32, (n_exp, tok), 0)
+    listed_t = jnp.zeros((n_exp, tok), F32)
+    for i in range(ids_ref.shape[0]):
+        listed_t = listed_t + jnp.where(exp_row == ids_ref[i:i + 1, :], 1.0, 0.0)
+    listed_t = listed_t.astype(BF16)
+    row, col = lax.broadcasted_iota(jnp.int32, (tok, tok), 0), lax.broadcasted_iota(jnp.int32, (tok, tok), 1)
+    listed = lax.dot_general(jnp.where(row == col, 1.0, 0.0).astype(BF16), listed_t, across, preferred_element_type=F32)
+    slots = lax.dot_general(jnp.where(row >= col, 1.0, 0.0).astype(BF16), listed_t, across, preferred_element_type=F32) * listed
     chosen = gate * listed
     table_ref[:, :n_exp] = ROUTE_SCALE * chosen / jnp.sum(chosen, axis=1, keepdims=True)
     table_ref[:, n_exp:] = slots
@@ -163,9 +183,8 @@
     seq, rope_dim = rope_cache.shape[1:]
     n_exp = w_router.shape[1]
     blocks = n_heads // GROUP
-    inv_freq = ROPE_BASE ** (-(2.0 * jnp.arange(rope_dim // 2)) / rope_dim)
-    angle = tok_pos.astype(F32)[:, None] * inv_freq[None, :]
-    trig = jnp.concatenate([jnp.cos(angle), jnp.sin(angle)], axis=1)
+    inv_freq = ROPE_BASE ** (-(2.0 * np.arange(rope_dim // 2)) / rope_dim)
+    freq = jnp.asarray(inv_freq[None, :].astype(np.float32))
     vmem = pl.BlockSpec(memory_space=pltpu.VMEM)
     hbm = pl.BlockSpec(memory_space=pl.ANY)
     dma = pltpu.SemaphoreType.DMA
@@ -182,22 +201,24 @@
         out_specs=[vmem, vmem, vmem, hbm, hbm],
         scratch_shapes=[
             pltpu.VMEM((blocks, dim, w_query.shape[1] // blocks), BF16),
-            pltpu.VMEM(w_kvdown.shape, BF16),
+            pltpu.VMEM(w_kvdown.shape[::-1], BF16),
             pltpu.VMEM(w_ukey.shape, BF16),
             pltpu.VMEM(w_uval.shape, BF16),
             pltpu.VMEM(w_out.shape, BF16),
-            pltpu.VMEM(w_router.shape, BF16),
+            pltpu.VMEM(w_router.shape[::-1], BF16),
             pltpu.VMEM(lat_cache.shape, BF16),
             pltpu.VMEM(rope_cache.shape, BF16),
             pltpu.VMEM((rank // LANES, tok * n_heads, LANES), F32),
             pltpu.VMEM((1, tok * n_heads, LANES), F32),
             pltpu.VMEM((rank // LANES, tok * n_heads, LANES), F32),
             pltpu.VMEM((tok, w_out.shape[0]), BF16),
+            pltpu.VMEM((tok // GROUP, GROUP * n_heads, GROUP * seq), F32),
+            pltpu.VMEM((tok // GROUP, GROUP * n_heads, GROUP * seq), BF16),
             dma((blocks,)), dma((5,)), dma((2,)), dma((2,)),
         ],
         compiler_params=pltpu.CompilerParams(vmem_limit_bytes=60000000),
         name='latent_attention',
-    )(tok_pos, tok_in, trig, expert_ids, attn_gain[None, :], ffn_gain[None, :], w_query, w_kvdown, w_ukey, w_uval, w_out, w_router, lat_cache, rope_cache)
+    )(tok_pos, tok_in, freq, expert_ids.T, attn_gain, ffn_gain, w_query, w_kvdown.T, w_ukey, w_uval, w_out, w_router.T, lat_cache, rope_cache)
 
 
 def moe_kernel(n_ep, n_exp, h_ref, table_ref, resid_ref, rowpat_ref, colpat_ref,
@@ -215,7 +236,7 @@
     rows_all = e_loc * rows_exp
     rows_q = e_loc * rows_par
     cw = dim // CHUNKS
-    half_dim = dim // 2
+    part_dim = dim // PARTS
 
     me = lax.axis_index('ep')
     z = me // 2
@@ -277,13 +298,13 @@
         return pltpu.make_async_remote_copy(src_ref=src, dst_ref=dst, send_sem=send, recv_sem=recv,
                                             device_id={'ep': dev}, device_id_type=MESH)
 
-    def h_hop(way, step, half):
+    def h_hop(way, step, part):
         dev = up_dev if way == 0 else dn_dev
         origin = chip(-step if way == 0 else step)
         slot = slot_of(par, origin)
-        cols = pl.ds(half * half_dim, half_dim)
+        cols = pl.ds(part * part_dim, part_dim)
         src = h_ref.at[:, cols] if step == 0 else hall.at[slot, :, cols]
-        return remote(src, hall.at[slot, :, cols], ag_send.at[way, step, half], ag_recv.at[way, step, half], dev)
+        return remote(src, hall.at[slot, :, cols], ag_send.at[way, step, part], ag_recv.at[way, step, part], dev)
 
     def t_hop(way, step):
         dev = up_dev if way == 0 else dn_dev
@@ -303,6 +324,35 @@
         return remote(src, gall.at[slot], ts_send.at[k], ts_recv.at[k], sib)
 
     t_steps = (far, far - 1)
+
+    def place_rows():
+        rowpat = rowpat_ref[...]
+        row_exp, row_dev, row_slot = rowpat[:, 0:1], rowpat[:, 1:2], rowpat[:, 2:3]
+        base = n_exp + e_loc * me
+        lane = lax.broadcasted_iota(jnp.int32, (rows_all, LANES), 1)
+        pick = jnp.where(lane == base + row_exp.astype(jnp.int32), 1.0, 0.0).astype(BF16)
+        slots_by_row = lax.dot_general(pick, gall[...].reshape(n_ep * tok, LANES).astype(BF16), (((1,), (1,)), ((), ())),
+                                       preferred_element_type=F32)
+        tok_dev = (lax.broadcasted_iota(jnp.int32, (rows_all, n_ep * tok), 1) // tok).astype(F32)
+        return jnp.where((slots_by_row == row_slot) & (tok_dev == row_dev), 1.0, 0.0).astype(BF16)
+
+    def combine_weights():
+        colpat = colpat_ref[...]
+        col_exp, col_chip, col_slot = colpat[0:1, :], colpat[1:2, :], colpat[2:3, :]
+        g_own = gall[pl.ds(par * nz, nz)].reshape(nz * tok, LANES)
+        part1 = g_own.astype(BF16)
+        rest1 = g_own - part1.astype(F32)
+        part2 = rest1.astype(BF16)
+        part3 = (rest1 - part2.astype(F32)).astype(BF16)
+        sub = lax.broadcasted_iota(jnp.int32, (LANES, rows_q), 0)
+        tok_chip = (lax.broadcasted_iota(jnp.int32, (nz * tok, rows_q), 0) // tok).astype(F32)
+        for q in range(2):
+            ids = e_loc * (me if q == 0 else sib) + col_exp.astype(jnp.int32)
+            sel_w = jnp.where(sub == ids, 1.0, 0.0).astype(BF16)
+            sel_s = jnp.where(sub == n_exp + ids, 1.0, 0.0).astype(BF16)
+            here = (dot32(part1, sel_s) == col_slot) & (tok_chip == col_chip)
+            for i, part in enumerate((part1, part2, part3)):
+                cmat[q, i] = jnp.where(here, dot32(part, sel_w), 0.0).astype(BF16)
     sent = []
 
     def go(copy):
@@ -311,12 +361,16 @@
         return copy
 
     hops, thops = {}, {}
+
+    def goes(way, step, part):
+        return step < far - 1 or part // (PARTS // 2) == way
+
     for way in range(2):
         thops[way, 0] = go(t_hop(way, 0))
-    for half in range(2):
+    for part in range(PARTS):
         for way in range(2):
-            hops[way, 0, half] = go(h_hop(way, 0, half))
-    crossed = [go(t_cross(0, z)), go(h_cross(0, z))]
+            hops[way, 0, part] = go(h_hop(way, 0, part))
+    t_crossed, h_crossed = [go(t_cross(0, z))], [go(h_cross(0, z))]
     hall[slot_of(par, z)] = h_ref[...]
     gall[slot_of(par, z)] = table_ref[...]
     for step in range(far):
@@ -326,49 +380,27 @@
                 thops[way, step].wait_recv()
                 if step + 1 < t_steps[way]:
                     thops[way, step + 1] = go(t_hop(way, step + 1))
-                crossed.append(go(t_cross(1 + 2 * step + way, origin)))
-        for half in range(2):
+                t_crossed.append(go(t_cross(1 + 2 * step + way, origin)))
+        if step == far - 1:
+            for copy in t_crossed:
+                copy.wait_recv()
+            place = place_rows()
+            combine_weights()
+        for part in range(PARTS):
             for way in range(2):
-                if step < far - 1 or half == way:
-                    hops[way, step, half].wait_recv()
-                if step < far - 2 or (step == far - 2 and half == way):
-                    hops[way, step + 1, half] = go(h_hop(way, step + 1, half))
+                if goes(way, step, part):
+                    hops[way, step, part].wait_recv()
+                    if step + 1 < far and goes(way, step + 1, part):
+                        hops[way, step + 1, part] = go(h_hop(way, step + 1, part))
         if step < far - 1:
             for way in range(2):
-                crossed.append(go(h_cross(1 + 2 * step + way, chip(-(step + 1) if way == 0 else step + 1))))
-    crossed.append(go(h_cross(2 * far - 1, chip(far))))
-    for copy in crossed:
+                h_crossed.append(go(h_cross(1 + 2 * step + way, chip(-(step + 1) if way == 0 else step + 1))))
+    h_crossed.append(go(h_cross(2 * far - 1, chip(far))))
+    for copy in h_crossed:
         copy.wait_recv()
-
-    rowpat = rowpat_ref[...]
-    row_exp, row_dev, row_slot = rowpat[:, 0:1], rowpat[:, 1:2], rowpat[:, 2:3]
-    base = n_exp + e_loc * me
-    lane = lax.broadcasted_iota(jnp.int32, (rows_all, LANES), 1)
-    pick = jnp.where(lane == base + row_exp.astype(jnp.int32), 1.0, 0.0).astype(BF16)
-    slots_by_row = lax.dot_general(pick, gall[...].reshape(n_ep * tok, LANES).astype(BF16), (((1,), (1,)), ((), ())),
-                                   preferred_element_type=F32)
-    tok_dev = (lax.broadcasted_iota(jnp.int32, (rows_all, n_ep * tok), 1) // tok).astype(F32)
-    place = jnp.where((slots_by_row == row_slot) & (tok_dev == row_dev), 1.0, 0.0).astype(BF16)
     for start, width in wide_tiles(dim, 256):
         rows = hall[:, :, start:start + width].reshape(n_ep * tok, width)
         xg[:, :, start:start + width] = dot32(place, rows).astype(BF16).reshape(e_loc, rows_exp, width)
-
-    colpat = colpat_ref[...]
-    col_exp, col_chip, col_slot = colpat[0:1, :], colpat[1:2, :], colpat[2:3, :]
-    g_own = gall[pl.ds(par * nz, nz)].reshape(nz * tok, LANES)
-    part1 = g_own.astype(BF16)
-    rest1 = g_own - part1.astype(F32)
-    part2 = rest1.astype(BF16)
-    part3 = (rest1 - part2.astype(F32)).astype(BF16)
-    sub = lax.broadcasted_iota(jnp.int32, (LANES, rows_q), 0)
-    tok_chip = (lax.broadcasted_iota(jnp.int32, (nz * tok, rows_q), 0) // tok).astype(F32)
-    for q in range(2):
-        ids = e_loc * (me if q == 0 else sib) + col_exp.astype(jnp.int32)
-        sel_w = jnp.where(sub == ids, 1.0, 0.0).astype(BF16)
-        sel_s = jnp.where(sub == n_exp + ids, 1.0, 0.0).astype(BF16)
-        here = (dot32(part1, sel_s) == col_slot) & (tok_chip == col_chip)
-        for i, part in enumerate((part1, part2, part3)):
-            cmat[q, i] = jnp.where(here, dot32(part, sel_w), 0.0).astype(BF16)
 
     def swiglu_tile(x, slot_g, slot_u, start, width):
         gate = dot32(x, wa[slot_g, :, start:start + width])
@@ -484,16 +516,13 @@
     combine(0)
     down(2)
     combine(1)
-    advance(0, 1)
     down(3)
     combine(2)
-    advance(1, 1)
-    advance(0, 2)
     combine(3)
     tiles = len(wide_tiles(ff, 256))
     pieces = [functools.partial(shared_up, hf, tile) for hf in range(halves) for tile in range(tiles)]
     pieces += [functools.partial(shared_down, j) for j in range(CHUNKS)]
-    events = [(2, 1), (1, 2), (3, 1), (0, 3), (2, 2), (1, 3), (3, 2), (2, 3), (3, 3)]
+    events = [(j, step) for step in range(1, far) for j in range(CHUNKS)]
     for i, event in enumerate(events):
         advance(*event)
         for piece in pieces[i * len(pieces) // len(events):(i + 1) * len(pieces) // len(events)]:
@@ -549,7 +578,7 @@
             pltpu.VMEM((SLOTS_B, ff, cw), BF16),
             pltpu.VMEM((tok, dim), F32),
             dma((2 * (e_loc + halves),)), dma((CHUNKS * (e_loc + halves),)),
-            dma((2, far, 2)), dma((2, far, 2)), dma((nz,)), dma((nz,)),
+            dma((2, far, PARTS)), dma((2, far, PARTS)), dma((nz,)), dma((nz,)),
             dma((2, far)), dma((2, far)), dma((nz,)), dma((nz,)),
             dma((CHUNKS,)), dma((CHUNKS,)),
             dma((2, CHUNKS, far)), dma((2, CHUNKS, far)),

time: 99.9 us -> 80.9 us (0.81)
  the two profiles are of different devices: /device:TPU:30 before, /device:TPU:21 now
where the time goes in v3:
time: 80.9 us; the launch traced here: 80.8 us
  Pallas kernels  78.6 us (97%)
  local copies, waits for them, and re-layouts  1.57 us (2%)
    pallas_call x1, Pallas kernels, moe_call(): pl.pallas_call(functools.partial(moe_kernel, n_ep, n_exp), out_shape=jax....  63.7 us
    pallas_call x1, Pallas kernels, attn_call(): pl.pallas_call(attn_kernel, out_shape=[jax.ShapeDtypeStruct((tok, dim), B...  14.8 us

profile of v3, /device:TPU:21, one launch (start us, length us, event | category | flops | bytes accessed | tf_op | source)
XLA Modules:
  0.0 80.8 jit_solution(12671247785901390553)
XLA Ops:
  0.6 14.8 %latent_attention.1 = (bf16[32,2048]{1,0:T(8,128)(2,1)}, bf16[32,2048]{1,0:T(8,128)(2,1)}, f32[32,128]{1,0:T(8,128)}, bf16[32,64,512]{2,1,0:T(8,128)(2,1)}, bf16[32,64,64]{2,1,0:T(8,128)(2,1)}) custom-call(s32[32]{0:T(128)} %pos_ref.1, bf16[32,2048]{1,0:T(8,128)(2,1)} %x_ref.1, f32[1,32]{1,0:T(1,128)} %constant.6.clone.freq_ref, s32[6,32]{1,0:T(8,128)} %bitcast.5, ...), custom_call_target="tpu_custom_call" | custom-call | tf_op jit(solution)/shard_map/latent_attention/pallas_call | solution.py:191
  15.5 63.7 %moe_ring.1 = bf16[32,2048]{1,0:T(8,128)(2,1)} custom-call(bf16[32,2048]{1,0:T(8,128)(2,1)} %get-tuple-element.8.h_ref, f32[32,128]{1,0:T(8,128)} %get-tuple-element.9.table_ref, bf16[32,2048]{1,0:T(8,128)(2,1)} %get-tuple-element.10.resid_ref, f32[384,8]{1,0:T(8,128)} %constant.7.clone.rowpat_ref, f32[8,192]{1,0:T(8,128)} %constant.8.clone.colpat_ref, ...), custom_call_target="tpu_custom_call" | custom-call | tf_op jit(solution)/shard_map/moe_ring/pallas_call | solution.py:561
  79.2 1.6 %copy.26 = bf16[32,2048]{1,0:T(8,128)(2,1)} copy(bf16[32,2048]{1,0:T(8,128)(2,1)} %moe_ring.1) | data formatting | bytes 262144

commit v4 on v3

--- a/solution.py
+++ b/solution.py
@@ -15,6 +15,8 @@
 F32 = jnp.float32
 BF16 = jnp.bfloat16
 CHUNKS = 4
+RINGS = 8
+TILE = 256
 SLOTS_A = 7
 SLOTS_B = 4
 CAP = 6
@@ -54,13 +56,14 @@
     kv_copy = pltpu.make_async_copy(wkv_ref, wkv, sem_w.at[0])
     uk_copy = pltpu.make_async_copy(uk_ref, uk, sem_w.at[1])
     uv_copy = pltpu.make_async_copy(uv_ref, uv, sem_w.at[2])
-    wo_copy = pltpu.make_async_copy(wo_ref, wo, sem_w.at[3])
-    wr_copy = pltpu.make_async_copy(wr_ref, wr, sem_w.at[4])
+    wo_copies = [pltpu.make_async_copy(wo_ref.at[:, pl.ds(i * dim // 2, dim // 2)], wo.at[i], sem_w.at[3 + i]) for i in range(2)]
+    wr_copy = pltpu.make_async_copy(wr_ref, wr, sem_w.at[5])
     lat_copy = pltpu.make_async_copy(lat_ref, lat, sem_c.at[0])
     rope_copy = pltpu.make_async_copy(rope_ref, rope, sem_c.at[1])
     kv_copy.start()
     q_copy(0).start()
     uk_copy.start()
+    q_copy(1).start()
 
     x = x_ref[...].astype(F32)
     x_norm = (unit_norm(x) * ag_ref[...].astype(F32).reshape(1, dim)).astype(BF16)
@@ -76,9 +79,8 @@
         return jnp.concatenate([first * cos - second * sin, second * cos + first * sin], axis=1)
 
     kv_copy.wait()
-    q_copy(1).start()
-    if blocks > 2:
-        q_copy(2).start()
+    for blk in range(2, blocks):
+        q_copy(blk).start()
     kv = lax.dot_general(x_norm, wkv[...], across, preferred_element_type=F32)
     lat_new = unit_norm(kv[:, :rank]).astype(BF16).astype(F32)
     rope_new = rotate(kv[:, rank:rank + half], kv[:, rank + half:]).astype(BF16).astype(F32)
@@ -93,13 +95,11 @@
         if blk == 0:
             lat_copy.start()
             rope_copy.start()
-            if blocks > 3:
-                q_copy(3).start()
+            uv_copy.start()
         elif blk == 1:
-            uv_copy.start()
             wr_copy.start()
-        if blk == blocks - 2:
-            wo_copy.start()
+            for copy in wo_copies:
+                copy.start()
         q = dot32(x_norm, wq[blk]).astype(BF16)
         for i in range(GROUP):
             n = blk * GROUP + i
@@ -153,11 +153,12 @@
     for n in range(n_heads):
         o_n = jnp.concatenate([o_lat[c, pl.ds(n, tok, stride=n_heads), :] for c in range(rank // LANES)], axis=1).astype(BF16)
         o_heads[:, n * uv.shape[2]:(n + 1) * uv.shape[2]] = dot32(o_n, uv[n]).astype(BF16)
+    for i, copy in enumerate(wo_copies):
+        copy.wait()
+        for start, width in wide_tiles(dim // 2, 512):
+            cols = slice(i * dim // 2 + start, i * dim // 2 + start + width)
+            res_ref[:, cols] = (x[:, cols] + dot32(o_heads[...], wo[i, :, start:start + width])).astype(BF16)
     wr_copy.wait()
-    wo_copy.wait()
-    for start, width in wide_tiles(dim, 512):
-        attn = dot32(o_heads[...], wo[:, start:start + width])
-        res_ref[:, start:start + width] = (x[:, start:start + width] + attn).astype(BF16)
     h = (unit_norm(res_ref[...].astype(F32)) * fg_ref[...].astype(F32).reshape(1, dim)).astype(BF16)
     h_ref[...] = h
 
@@ -204,7 +205,7 @@
             pltpu.VMEM(w_kvdown.shape[::-1], BF16),
             pltpu.VMEM(w_ukey.shape, BF16),
             pltpu.VMEM(w_uval.shape, BF16),
-            pltpu.VMEM(w_out.shape, BF16),
+            pltpu.VMEM((2, w_out.shape[0], dim // 2), BF16),
             pltpu.VMEM(w_router.shape[::-1], BF16),
             pltpu.VMEM(lat_cache.shape, BF16),
             pltpu.VMEM(rope_cache.shape, BF16),
@@ -214,7 +215,7 @@
             pltpu.VMEM((tok, w_out.shape[0]), BF16),
             pltpu.VMEM((tok // GROUP, GROUP * n_heads, GROUP * seq), F32),
             pltpu.VMEM((tok // GROUP, GROUP * n_heads, GROUP * seq), BF16),
-            dma((blocks,)), dma((5,)), dma((2,)), dma((2,)),
+            dma((blocks,)), dma((6,)), dma((2,)), dma((2,)),
         ],
         compiler_params=pltpu.CompilerParams(vmem_limit_bytes=60000000),
         name='latent_attention',
@@ -236,6 +237,8 @@
     rows_all = e_loc * rows_exp
     rows_q = e_loc * rows_par
     cw = dim // CHUNKS
+    rw = dim // RINGS
+    subs = RINGS // CHUNKS
     part_dim = dim // PARTS
 
     me = lax.axis_index('ep')
@@ -412,7 +415,7 @@
         slot_u = lax.rem(2 * e + 1, SLOTS_A)
         for unit, slot in ((2 * e, slot_g), (2 * e + 1, slot_u)):
             pltpu.make_async_copy(eg_ref.at[0], wa.at[slot], sem_a.at[unit]).wait()
-        for start, width in wide_tiles(ff, 256):
+        for start, width in wide_tiles(ff, TILE):
             act[e, :, start:start + width] = swiglu_tile(xg[e], slot_g, slot_u, start, width)
         for e_st in range(e_loc):
             @pl.when(e == e_st)
@@ -446,13 +449,12 @@
 
     def combine(j):
         exch[j].wait_recv()
-        own = ebuf[j, par].reshape(rows_q, cw)
-        other = esib[j].reshape(rows_q, cw)
-        for start, width in wide_tiles(cw, 256):
-            total = dot32(cmat[0, 0], own[:, start:start + width]) + dot32(cmat[1, 0], other[:, start:start + width])
-            for i in (1, 2):
-                total += dot32(cmat[0, i], own[:, start:start + width]) + dot32(cmat[1, i], other[:, start:start + width])
-            ct[j, :, :, start:start + width] = total.reshape(nz, tok, width)
+        own = ebuf[j, par].reshape(rows_q, rw)
+        other = esib[j].reshape(rows_q, rw)
+        total = dot32(cmat[0, 0], own) + dot32(cmat[1, 0], other)
+        for i in (1, 2):
+            total += dot32(cmat[0, i], own) + dot32(cmat[1, i], other)
+        ct[j] = total.reshape(nz, tok, rw)
         for way in range(2):
             rcopies[way, j, 1] = go(ring_copy(way, j, 1))
 
@@ -466,23 +468,27 @@
                 rcopies[way, j, step + 1] = go(ring_copy(way, j, step + 1))
 
     def finish(j):
-        cols = slice(j * cw, (j + 1) * cw)
+        cols = slice(j * rw, (j + 1) * rw)
         total = resid_ref[:, cols].astype(F32) + sh_out[:, cols] + ct[j, z]
         for way in range(2):
             rcopies[way, j, reach(way, j)].wait_recv()
             total += ring[way, j, reach(way, j) - 1]
-        out_ref[:, cols] = total.astype(BF16)
+        out_ref[:, cols] = total
 
     exch = {}
 
-    def down(j):
+    def down(r):
+        j, sub = r // subs, r % subs
+        if sub == 0:
+            for e in range(e_loc):
+                b_copy(j * e_loc + e).wait()
         for e in range(e_loc):
-            b_copy(j * e_loc + e).wait()
-        for e in range(e_loc):
-            res = dot32(act[e], b_place(j * e_loc + e)[...]).astype(BF16)
-            ebuf[j, 0, e] = res[:rows_par]
-            ebuf[j, 1, e] = res[rows_par:]
-        exch[j] = go(remote(ebuf.at[j, 1 - par], esib.at[j], ex_send.at[j], ex_recv.at[j], sib))
+            res = dot32(act[e], b_place(j * e_loc + e)[:, sub * rw:(sub + 1) * rw]).astype(BF16)
+            ebuf[r, 0, e] = res[:rows_par]
+            ebuf[r, 1, e] = res[rows_par:]
+        exch[r] = go(remote(ebuf.at[r, 1 - par], esib.at[r], ex_send.at[r], ex_recv.at[r], sib))
+        if sub < subs - 1:
+            return
         shared = CHUNKS * e_loc
         if j == 1:
             a_copy(2 * e_loc + 1).start()
@@ -497,7 +503,7 @@
 
     def shared_up(hf, tile):
         unit = 2 * e_loc + 2 * hf
-        start, width = wide_tiles(ff, 256)[tile]
+        start, width = wide_tiles(ff, TILE)[tile]
         if tile == 0:
             a_copy(unit).wait()
             a_copy(unit + 1).wait()
@@ -513,21 +519,20 @@
 
     down(0)
     down(1)
-    combine(0)
-    down(2)
-    combine(1)
-    down(3)
-    combine(2)
-    combine(3)
-    tiles = len(wide_tiles(ff, 256))
+    for r in range(2, RINGS):
+        down(r)
+        combine(r - 2)
+    combine(RINGS - 2)
+    combine(RINGS - 1)
+    tiles = len(wide_tiles(ff, TILE))
     pieces = [functools.partial(shared_up, hf, tile) for hf in range(halves) for tile in range(tiles)]
     pieces += [functools.partial(shared_down, j) for j in range(CHUNKS)]
-    events = [(j, step) for step in range(1, far) for j in range(CHUNKS)]
+    events = [(j, step) for step in range(1, far) for j in range(RINGS)]
     for i, event in enumerate(events):
         advance(*event)
         for piece in pieces[i * len(pieces) // len(events):(i + 1) * len(pieces) // len(events)]:
             piece()
-    for j in range(CHUNKS):
+    for j in range(RINGS):
         finish(j)
     for copy in sent:
         copy.wait_send()
@@ -541,6 +546,7 @@
     halves = w_sg.shape[1] // ff
     far = nz // 2
     cw = dim // CHUNKS
+    rw = dim // RINGS
     rows_par = nz * CAP
     rows_exp = 2 * rows_par
     rows_all = e_loc * rows_exp
@@ -560,7 +566,7 @@
     dma = pltpu.SemaphoreType.DMA
     return pl.pallas_call(
         functools.partial(moe_kernel, n_ep, n_exp),
-        out_shape=jax.ShapeDtypeStruct((tok, dim), BF16),
+        out_shape=jax.ShapeDtypeStruct((tok, dim), F32),
         in_specs=[vmem] * 5 + [hbm] * 6,
         out_specs=vmem,
         scratch_shapes=[
@@ -569,23 +575,23 @@
             pltpu.VMEM((e_loc, rows_exp, dim), BF16),
             pltpu.VMEM((e_loc, rows_exp, ff), BF16),
             pltpu.VMEM((halves, tok, ff), BF16),
-            pltpu.VMEM((CHUNKS, 2, e_loc, rows_par, cw), BF16),
-            pltpu.VMEM((CHUNKS, e_loc, rows_par, cw), BF16),
+            pltpu.VMEM((RINGS, 2, e_loc, rows_par, rw), BF16),
+            pltpu.VMEM((RINGS, e_loc, rows_par, rw), BF16),
             pltpu.VMEM((2, 3, nz * tok, rows_q), BF16),
-            pltpu.VMEM((CHUNKS, nz, tok, cw), F32),
-            pltpu.VMEM((2, CHUNKS, far, tok, cw), F32),
+            pltpu.VMEM((RINGS, nz, tok, rw), F32),
+            pltpu.VMEM((2, RINGS, far, tok, rw), F32),
             pltpu.VMEM((SLOTS_A, dim, ff), BF16),
             pltpu.VMEM((SLOTS_B, ff, cw), BF16),
             pltpu.VMEM((tok, dim), F32),
             dma((2 * (e_loc + halves),)), dma((CHUNKS * (e_loc + halves),)),
             dma((2, far, PARTS)), dma((2, far, PARTS)), dma((nz,)), dma((nz,)),
             dma((2, far)), dma((2, far)), dma((nz,)), dma((nz,)),
-            dma((CHUNKS,)), dma((CHUNKS,)),
-            dma((2, CHUNKS, far)), dma((2, CHUNKS, far)),
+            dma((RINGS,)), dma((RINGS,)),
+            dma((2, RINGS, far)), dma((2, RINGS, far)),
         ],
         compiler_params=pltpu.CompilerParams(collective_id=0, has_side_effects=True, vmem_limit_bytes=67000000),
         name='moe_ring',
-    )(h_norm, table, resid, jnp.asarray(rowpat), jnp.asarray(colpat), w_sg, w_su, w_sd, w_eg, w_eu, w_ed)
+    )(h_norm, table, resid, jnp.asarray(rowpat), jnp.asarray(colpat), w_sg, w_su, w_sd, w_eg, w_eu, w_ed).astype(BF16)
 
 
 def solution(mesh):

time: 80.9 us -> 83.3 us (1.030)
  Pallas kernels: 78.6 us -> 80.8 us
  other arithmetic: 0 us -> 1.62 us
  local copies, waits for them, and re-layouts: 1.57 us -> 0 us
    pallas_call x1, Pallas kernels: 63.7 us -> 66.7 us  [moe_call(): pl.pallas_call(functools.partial(moe_kernel, n_ep, n_exp), out_shape=jax....]
    convert_element_type x0 -> x1, other arithmetic: none -> 1.62 us  [moe_call(): return pl.pallas_call(functools.partial(moe_kernel, n_ep, n_exp), out_sha...]
    unnamed x1 -> x0, local copies, waits for them, and re-layouts: 1.57 us -> none
where the time goes in v4:
time: 83.3 us; the launch traced here: 83.1 us
  Pallas kernels  80.8 us (97%)
  other arithmetic  1.62 us (2%)
    pallas_call x1, Pallas kernels, moe_call(): pl.pallas_call(functools.partial(moe_kernel, n_ep, n_exp), out_shape=jax....  66.7 us
    pallas_call x1, Pallas kernels, attn_call(): pl.pallas_call(attn_kernel, out_shape=[jax.ShapeDtypeStruct((tok, dim), B...  14.1 us

profile of v4, /device:TPU:21, one launch (start us, length us, event | category | flops | bytes accessed | tf_op | source)
XLA Modules:
  0.0 83.1 jit_solution(1160456943682078849)
XLA Ops:
  0.6 14.1 %latent_attention.1 = (bf16[32,2048]{1,0:T(8,128)(2,1)}, bf16[32,2048]{1,0:T(8,128)(2,1)}, f32[32,128]{1,0:T(8,128)}, bf16[32,64,512]{2,1,0:T(8,128)(2,1)}, bf16[32,64,64]{2,1,0:T(8,128)(2,1)}) custom-call(s32[32]{0:T(128)} %pos_ref.1, bf16[32,2048]{1,0:T(8,128)(2,1)} %x_ref.1, f32[1,32]{1,0:T(1,128)} %constant.6.clone.freq_ref, s32[6,32]{1,0:T(8,128)} %bitcast.5, ...), custom_call_target="tpu_custom_call" | custom-call | tf_op jit(solution)/shard_map/latent_attention/pallas_call | solution.py:192
  14.8 66.7 %moe_ring.1 = f32[32,2048]{1,0:T(8,128)} custom-call(bf16[32,2048]{1,0:T(8,128)(2,1)} %get-tuple-element.8.h_ref, f32[32,128]{1,0:T(8,128)} %get-tuple-element.9.table_ref, bf16[32,2048]{1,0:T(8,128)(2,1)} %get-tuple-element.10.resid_ref, f32[384,8]{1,0:T(8,128)} %constant.7.clone.rowpat_ref, f32[8,192]{1,0:T(8,128)} %constant.8.clone.colpat_ref, ...), custom_call_target="tpu_custom_call" | custom-call | tf_op jit(solution)/shard_map/moe_ring/pallas_call | solution.py:567
  81.5 1.6 %convert_element_type.3 = bf16[32,2048]{1,0:T(8,128)(2,1)} convert(f32[32,2048]{1,0:T(8,128)} %moe_ring.1) | non-fusion elementwise | flops 65536 | bytes 393216 | tf_op jit(solution)/shard_map/convert_element_type | solution.py:594

commit v5 on v3

--- a/solution.py
+++ b/solution.py
@@ -15,6 +15,8 @@
 F32 = jnp.float32
 BF16 = jnp.bfloat16
 CHUNKS = 4
+RINGS = 4
+TILE = 256
 SLOTS_A = 7
 SLOTS_B = 4
 CAP = 6
@@ -36,9 +38,9 @@
     return [(start, min(width, total - start)) for start in range(0, total, width)]
 
 
-def attn_kernel(pos_ref, x_ref, freq_ref, ids_ref, ag_ref, fg_ref, wq_ref, wkv_ref, uk_ref, uv_ref, wo_ref, wr_ref, lat_ref, rope_ref,
+def attn_kernel(pos_hbm, x_hbm, freq_hbm, ids_hbm, ag_hbm, fg_hbm, wq_ref, wkv_ref, uk_ref, uv_ref, wo_ref, wr_ref, lat_ref, rope_ref,
                 res_ref, h_ref, table_ref, lat_out, rope_out,
-                wq, wkv, uk, uv, wo, wr, lat, rope, q_lat, q_rope, o_lat, o_heads, score, prob, sem_q, sem_w, sem_c, sem_o):
+                wq, wkv, uk, uv, wo, wr, lat, rope, q_lat, q_rope, o_lat, o_heads, score, prob, pos_ref, x_ref, freq_ref, ids_ref, ag_ref, fg_ref, sem_q, sem_w, sem_c, sem_o, sem_i):
     n_heads, nope, rank = uk_ref.shape
     tok, dim = x_ref.shape
     seq, rope_dim = rope_ref.shape[1:]
@@ -54,13 +56,22 @@
     kv_copy = pltpu.make_async_copy(wkv_ref, wkv, sem_w.at[0])
     uk_copy = pltpu.make_async_copy(uk_ref, uk, sem_w.at[1])
     uv_copy = pltpu.make_async_copy(uv_ref, uv, sem_w.at[2])
-    wo_copy = pltpu.make_async_copy(wo_ref, wo, sem_w.at[3])
-    wr_copy = pltpu.make_async_copy(wr_ref, wr, sem_w.at[4])
+    wo_copies = [pltpu.make_async_copy(wo_ref.at[:, pl.ds(i * dim // 2, dim // 2)], wo.at[i], sem_w.at[3 + i]) for i in range(2)]
+    wr_copy = pltpu.make_async_copy(wr_ref, wr, sem_w.at[5])
     lat_copy = pltpu.make_async_copy(lat_ref, lat, sem_c.at[0])
     rope_copy = pltpu.make_async_copy(rope_ref, rope, sem_c.at[1])
+    small = [pltpu.make_async_copy(src, dst, sem_i.at[i]) for i, (src, dst) in enumerate((
+        (x_hbm, x_ref), (ag_hbm, ag_ref), (pos_hbm, pos_ref), (freq_hbm, freq_ref), (fg_hbm, fg_ref), (ids_hbm, ids_ref)))]
+    for copy in small[:4]:
+        copy.start()
     kv_copy.start()
     q_copy(0).start()
     uk_copy.start()
+    q_copy(1).start()
+    for copy in small[4:]:
+        copy.start()
+    for copy in small:
+        copy.wait()
 
     x = x_ref[...].astype(F32)
     x_norm = (unit_norm(x) * ag_ref[...].astype(F32).reshape(1, dim)).astype(BF16)
@@ -76,9 +87,8 @@
         return jnp.concatenate([first * cos - second * sin, second * cos + first * sin], axis=1)
 
     kv_copy.wait()
-    q_copy(1).start()
-    if blocks > 2:
-        q_copy(2).start()
+    for blk in range(2, blocks):
+        q_copy(blk).start()
     kv = lax.dot_general(x_norm, wkv[...], across, preferred_element_type=F32)
     lat_new = unit_norm(kv[:, :rank]).astype(BF16).astype(F32)
     rope_new = rotate(kv[:, rank:rank + half], kv[:, rank + half:]).astype(BF16).astype(F32)
@@ -86,6 +96,18 @@
     def spread(ref, n, val):
         for c in range(val.shape[1] // LANES):
             ref[c, pl.ds(n, tok, stride=n_heads), :] = val[:, c * LANES:(c + 1) * LANES]
+
+    queries = []
+
+    def heads(blk):
+        q = queries[blk]
+        for i in range(GROUP):
+            n = blk * GROUP + i
+            at = i * head
+            spread(q_lat, n, dot32(q[:, at:at + nope], uk[n]).astype(BF16).astype(F32))
+            q_r = q[:, at + nope:at + head].astype(F32)
+            q_r = rotate(q_r[:, :half], q_r[:, half:]).astype(BF16).astype(F32)
+            spread(q_rope, n, jnp.concatenate([q_r, jnp.zeros((tok, LANES - rope_dim), F32)], axis=1))
 
     uk_copy.wait()
     for blk in range(blocks):
@@ -93,24 +115,17 @@
         if blk == 0:
             lat_copy.start()
             rope_copy.start()
-            if blocks > 3:
-                q_copy(3).start()
+            uv_copy.start()
         elif blk == 1:
-            uv_copy.start()
             wr_copy.start()
-        if blk == blocks - 2:
-            wo_copy.start()
-        q = dot32(x_norm, wq[blk]).astype(BF16)
-        for i in range(GROUP):
-            n = blk * GROUP + i
-            at = i * head
-            q_n = dot32(q[:, at:at + nope], uk[n]).astype(BF16).astype(F32)
-            spread(q_lat, n, q_n)
-            q_r = q[:, at + nope:at + head].astype(F32)
-            q_r = rotate(q_r[:, :half], q_r[:, half:]).astype(BF16).astype(F32)
-            spread(q_rope, n, jnp.concatenate([q_r, jnp.zeros((tok, LANES - rope_dim), F32)], axis=1))
+            for copy in wo_copies:
+                copy.start()
+        queries.append(dot32(x_norm, wq[blk]).astype(BF16))
+        if blk > 0:
+            heads(blk - 1)
     lat_copy.wait()
     rope_copy.wait()
+    heads(blocks - 1)
     rows, keys = GROUP * n_heads, GROUP * seq
     key = lax.broadcasted_iota(jnp.int32, (rows, keys), 1)
     same = (key // seq) == (lax.broadcasted_iota(jnp.int32, (rows, keys), 0) // n_heads)
@@ -153,11 +168,12 @@
     for n in range(n_heads):
         o_n = jnp.concatenate([o_lat[c, pl.ds(n, tok, stride=n_heads), :] for c in range(rank // LANES)], axis=1).astype(BF16)
         o_heads[:, n * uv.shape[2]:(n + 1) * uv.shape[2]] = dot32(o_n, uv[n]).astype(BF16)
+    for i, copy in enumerate(wo_copies):
+        copy.wait()
+        for start, width in wide_tiles(dim // 2, 512):
+            cols = slice(i * dim // 2 + start, i * dim // 2 + start + width)
+            res_ref[:, cols] = (x[:, cols] + dot32(o_heads[...], wo[i, :, start:start + width])).astype(BF16)
     wr_copy.wait()
-    wo_copy.wait()
-    for start, width in wide_tiles(dim, 512):
-        attn = dot32(o_heads[...], wo[:, start:start + width])
-        res_ref[:, start:start + width] = (x[:, start:start + width] + attn).astype(BF16)
     h = (unit_norm(res_ref[...].astype(F32)) * fg_ref[...].astype(F32).reshape(1, dim)).astype(BF16)
     h_ref[...] = h
 
@@ -197,14 +213,14 @@
             jax.ShapeDtypeStruct(lat_cache.shape, BF16),
             jax.ShapeDtypeStruct(rope_cache.shape, BF16),
         ],
-        in_specs=[pl.BlockSpec(memory_space=pltpu.SMEM)] + [vmem] * 5 + [hbm] * 8,
+        in_specs=[hbm] * 14,
         out_specs=[vmem, vmem, vmem, hbm, hbm],
         scratch_shapes=[
             pltpu.VMEM((blocks, dim, w_query.shape[1] // blocks), BF16),
             pltpu.VMEM(w_kvdown.shape[::-1], BF16),
             pltpu.VMEM(w_ukey.shape, BF16),
             pltpu.VMEM(w_uval.shape, BF16),
-            pltpu.VMEM(w_out.shape, BF16),
+            pltpu.VMEM((2, w_out.shape[0], dim // 2), BF16),
             pltpu.VMEM(w_router.shape[::-1], BF16),
             pltpu.VMEM(lat_cache.shape, BF16),
             pltpu.VMEM(rope_cache.shape, BF16),
@@ -214,21 +230,27 @@
             pltpu.VMEM((tok, w_out.shape[0]), BF16),
             pltpu.VMEM((tok // GROUP, GROUP * n_heads, GROUP * seq), F32),
             pltpu.VMEM((tok // GROUP, GROUP * n_heads, GROUP * seq), BF16),
-            dma((blocks,)), dma((5,)), dma((2,)), dma((2,)),
+            pltpu.SMEM(tok_pos.shape, jnp.int32),
+            pltpu.VMEM((tok, dim), BF16),
+            pltpu.VMEM(freq.shape, F32),
+            pltpu.VMEM(expert_ids.shape[::-1], jnp.int32),
+            pltpu.VMEM((dim,), BF16),
+            pltpu.VMEM((dim,), BF16),
+            dma((blocks,)), dma((6,)), dma((2,)), dma((2,)), dma((6,)),
         ],
         compiler_params=pltpu.CompilerParams(vmem_limit_bytes=60000000),
         name='latent_attention',
     )(tok_pos, tok_in, freq, expert_ids.T, attn_gain, ffn_gain, w_query, w_kvdown.T, w_ukey, w_uval, w_out, w_router.T, lat_cache, rope_cache)
 
 
-def moe_kernel(n_ep, n_exp, h_ref, table_ref, resid_ref, rowpat_ref, colpat_ref,
-               sg_ref, su_ref, sd_ref, eg_ref, eu_ref, ed_ref, out_ref,
+def moe_kernel(n_ep, n_exp, h_hbm, table_hbm, resid_hbm, rowpat_hbm, colpat_hbm,
+               sg_ref, su_ref, sd_ref, eg_ref, eu_ref, ed_ref, out_hbm,
                hall, gall, xg, act, act_sh, ebuf, esib, cmat, ct, ring, wa, wb, sh_out,
                sem_a, sem_b, ag_send, ag_recv, sib_send, sib_recv, tb_send, tb_recv, ts_send, ts_recv,
-               ex_send, ex_recv, rg_send, rg_recv):
+               ex_send, ex_recv, rg_send, rg_recv, h_ref, table_ref, resid_ref, rowpat_ref, colpat_ref, out_ref, sem_i, sem_o):
     nz = n_ep // 2
     far = nz // 2
-    tok, dim = h_ref.shape
+    tok, dim = h_hbm.shape
     e_loc, _, ff = eg_ref.shape
     halves = sg_ref.shape[1] // ff
     rows_par = nz * CAP
@@ -236,6 +258,8 @@
     rows_all = e_loc * rows_exp
     rows_q = e_loc * rows_par
     cw = dim // CHUNKS
+    rw = dim // RINGS
+    subs = RINGS // CHUNKS
     part_dim = dim // PARTS
 
     me = lax.axis_index('ep')
@@ -284,14 +308,20 @@
             src = sd_ref.at[pl.ds(hf * ff, ff), pl.ds(j * cw, cw)]
         return pltpu.make_async_copy(src, b_place(unit), sem_b.at[unit])
 
+    small = [pltpu.make_async_copy(src, dst, sem_i.at[i]) for i, (src, dst) in enumerate((
+        (table_hbm, table_ref), (h_hbm, h_ref), (resid_hbm, resid_ref), (rowpat_hbm, rowpat_ref), (colpat_hbm, colpat_ref)))]
+    for copy in small:
+        copy.start()
+
+    barrier = pltpu.get_barrier_semaphore()
+    for dev in (up_dev, dn_dev, sib):
+        pl.semaphore_signal(barrier, inc=1, device_id={'ep': dev}, device_id_type=MESH)
     for unit in range(SLOTS_A):
         a_copy(unit).start()
     for unit in range(SLOTS_B):
         b_copy(unit).start()
-
-    barrier = pltpu.get_barrier_semaphore()
-    for dev in (up_dev, dn_dev, sib):
-        pl.semaphore_signal(barrier, inc=1, device_id={'ep': dev}, device_id_type=MESH)
+    for copy in small:
+        copy.wait()
     pl.semaphore_wait(barrier, 3)
 
     def remote(src, dst, send, recv, dev):
@@ -412,7 +442,7 @@
         slot_u = lax.rem(2 * e + 1, SLOTS_A)
         for unit, slot in ((2 * e, slot_g), (2 * e + 1, slot_u)):
             pltpu.make_async_copy(eg_ref.at[0], wa.at[slot], sem_a.at[unit]).wait()
-        for start, width in wide_tiles(ff, 256):
+        for start, width in wide_tiles(ff, TILE):
             act[e, :, start:start + width] = swiglu_tile(xg[e], slot_g, slot_u, start, width)
         for e_st in range(e_loc):
             @pl.when(e == e_st)
@@ -439,7 +469,7 @@
         dev = up_dev if way == 0 else dn_dev
         ahead = reach(way, j) - step + 1
         dest = chip(ahead if way == 0 else -ahead)
-        src = ct.at[j, dest] if step == 1 else ring.at[way, j, step - 2]
+        src = ct.at[j // subs, dest, :, pl.ds(j % subs * rw, rw)] if step == 1 else ring.at[way, j, step - 2]
         return remote(src, ring.at[way, j, step - 1], rg_send.at[way, j, step - 1], rg_recv.at[way, j, step - 1], dev)
 
     rcopies = {}
@@ -453,8 +483,9 @@
             for i in (1, 2):
                 total += dot32(cmat[0, i], own[:, start:start + width]) + dot32(cmat[1, i], other[:, start:start + width])
             ct[j, :, :, start:start + width] = total.reshape(nz, tok, width)
-        for way in range(2):
-            rcopies[way, j, 1] = go(ring_copy(way, j, 1))
+        for r in range(j * subs, (j + 1) * subs):
+            for way in range(2):
+                rcopies[way, r, 1] = go(ring_copy(way, r, 1))
 
     def advance(j, step):
         for way in range(2):
@@ -462,16 +493,19 @@
                 rcopies[way, j, step].wait_recv()
                 ahead = reach(way, j) - step
                 dest = chip(ahead if way == 0 else -ahead)
-                ring[way, j, step - 1] += ct[j, dest]
+                ring[way, j, step - 1] += ct[j // subs, dest, :, j % subs * rw:(j % subs + 1) * rw]
                 rcopies[way, j, step + 1] = go(ring_copy(way, j, step + 1))
 
     def finish(j):
-        cols = slice(j * cw, (j + 1) * cw)
-        total = resid_ref[:, cols].astype(F32) + sh_out[:, cols] + ct[j, z]
+        cols = slice(j * rw, (j + 1) * rw)
+        total = resid_ref[:, cols].astype(F32) + sh_out[:, cols] + ct[j // subs, z, :, j % subs * rw:(j % subs + 1) * rw]
         for way in range(2):
             rcopies[way, j, reach(way, j)].wait_recv()
             total += ring[way, j, reach(way, j) - 1]
         out_ref[:, cols] = total.astype(BF16)
+        back = pltpu.make_async_copy(out_ref.at[:, pl.ds(j * rw, rw)], out_hbm.at[:, pl.ds(j * rw, rw)], sem_o.at[j])
+        back.start()
+        return back
 
     exch = {}
 
@@ -497,7 +531,7 @@
 
     def shared_up(hf, tile):
         unit = 2 * e_loc + 2 * hf
-        start, width = wide_tiles(ff, 256)[tile]
+        start, width = wide_tiles(ff, TILE)[tile]
         if tile == 0:
             a_copy(unit).wait()
             a_copy(unit + 1).wait()
@@ -519,18 +553,25 @@
     down(3)
     combine(2)
     combine(3)
-    tiles = len(wide_tiles(ff, 256))
+    tiles = len(wide_tiles(ff, TILE))
     pieces = [functools.partial(shared_up, hf, tile) for hf in range(halves) for tile in range(tiles)]
     pieces += [functools.partial(shared_down, j) for j in range(CHUNKS)]
-    events = [(j, step) for step in range(1, far) for j in range(CHUNKS)]
+    events = [(j, step) for step in range(1, far) for j in range(RINGS)]
+    early = list(sent)
+    gone = 0
     for i, event in enumerate(events):
+        until = (i + 1) * len(early) // len(events)
+        for copy in early[gone:until]:
+            copy.wait_send()
+        gone = until
         advance(*event)
         for piece in pieces[i * len(pieces) // len(events):(i + 1) * len(pieces) // len(events)]:
             piece()
-    for j in range(CHUNKS):
-        finish(j)
-    for copy in sent:
+    backs = [finish(j) for j in range(RINGS)]
+    for copy in sent[len(early):]:
         copy.wait_send()
+    for back in backs:
+        back.wait()
 
 
 def moe_call(n_ep, h_norm, table, resid, w_sg, w_su, w_sd, w_eg, w_eu, w_ed):
@@ -541,6 +582,7 @@
     halves = w_sg.shape[1] // ff
     far = nz // 2
     cw = dim // CHUNKS
+    rw = dim // RINGS
     rows_par = nz * CAP
     rows_exp = 2 * rows_par
     rows_all = e_loc * rows_exp
@@ -555,14 +597,13 @@
     colpat[0] = col // rows_par
     colpat[1] = (col % rows_par) // CAP
     colpat[2] = col % CAP + 1
-    vmem = pl.BlockSpec(memory_space=pltpu.VMEM)
     hbm = pl.BlockSpec(memory_space=pl.ANY)
     dma = pltpu.SemaphoreType.DMA
     return pl.pallas_call(
         functools.partial(moe_kernel, n_ep, n_exp),
         out_shape=jax.ShapeDtypeStruct((tok, dim), BF16),
-        in_specs=[vmem] * 5 + [hbm] * 6,
-        out_specs=vmem,
+        in_specs=[hbm] * 11,
+        out_specs=hbm,
         scratch_shapes=[
             pltpu.VMEM((n_ep, tok, dim), BF16),
             pltpu.VMEM((n_ep, tok, LANES), F32),
@@ -573,7 +614,7 @@
             pltpu.VMEM((CHUNKS, e_loc, rows_par, cw), BF16),
             pltpu.VMEM((2, 3, nz * tok, rows_q), BF16),
             pltpu.VMEM((CHUNKS, nz, tok, cw), F32),
-            pltpu.VMEM((2, CHUNKS, far, tok, cw), F32),
+            pltpu.VMEM((2, RINGS, far, tok, rw), F32),
             pltpu.VMEM((SLOTS_A, dim, ff), BF16),
             pltpu.VMEM((SLOTS_B, ff, cw), BF16),
             pltpu.VMEM((tok, dim), F32),
@@ -581,7 +622,14 @@
             dma((2, far, PARTS)), dma((2, far, PARTS)), dma((nz,)), dma((nz,)),
             dma((2, far)), dma((2, far)), dma((nz,)), dma((nz,)),
             dma((CHUNKS,)), dma((CHUNKS,)),
-            dma((2, CHUNKS, far)), dma((2, CHUNKS, far)),
+            dma((2, RINGS, far)), dma((2, RINGS, far)),
+            pltpu.VMEM((tok, dim), BF16),
+            pltpu.VMEM((tok, LANES), F32),
+            pltpu.VMEM((tok, dim), BF16),
+            pltpu.VMEM(rowpat.shape, F32),
+            pltpu.VMEM(colpat.shape, F32),
+            pltpu.VMEM((tok, dim), BF16),
+            dma((5,)), dma((RINGS,)),
         ],
         compiler_params=pltpu.CompilerParams(collective_id=0, has_side_effects=True, vmem_limit_bytes=67000000),
         name='moe_ring',

time: 80.9 us -> 79 us (0.977)
  Pallas kernels: 78.6 us -> 76.6 us
    pallas_call x1, Pallas kernels: 63.7 us -> 62.6 us  [moe_call(): pl.pallas_call(functools.partial(moe_kernel, n_ep, n_exp), out_shape=jax....]
    pallas_call x1, Pallas kernels: 14.8 us -> 14 us  [attn_call(): pl.pallas_call(attn_kernel, out_shape=[jax.ShapeDtypeStruct((tok, dim), B...]
where the time goes in v5:
time: 79 us; the launch traced here: 78.8 us
  Pallas kernels  76.6 us (97%)
  local copies, waits for them, and re-layouts  1.57 us (2%)
    pallas_call x1, Pallas kernels, moe_call(): pl.pallas_call(functools.partial(moe_kernel, n_ep, n_exp), out_shape=jax....  62.6 us
    pallas_call x1, Pallas kernels, attn_call(): pl.pallas_call(attn_kernel, out_shape=[jax.ShapeDtypeStruct((tok, dim), B...  14 us

profile of v5, /device:TPU:21, one launch (start us, length us, event | category | flops | bytes accessed | tf_op | source)
XLA Modules:
  0.0 78.8 jit_solution(9453000739083660244)
XLA Ops:
  0.6 14.0 %latent_attention.1 = (bf16[32,2048]{1,0:T(8,128)(2,1)}, bf16[32,2048]{1,0:T(8,128)(2,1)}, f32[32,128]{1,0:T(8,128)}, bf16[32,64,512]{2,1,0:T(8,128)(2,1)}, bf16[32,64,64]{2,1,0:T(8,128)(2,1)}) custom-call(s32[32]{0:T(128)} %pos_hbm.1, bf16[32,2048]{1,0:T(8,128)(2,1)} %x_hbm.1, f32[1,32]{1,0:T(1,128)} %constant.6.clone.freq_hbm, s32[6,32]{1,0:T(8,128)} %bitcast.5, ...), custom_call_target="tpu_custom_call" | custom-call | tf_op jit(solution)/shard_map/latent_attention/pallas_call | solution.py:207
  14.7 62.6 %moe_ring.1 = bf16[32,2048]{1,0:T(8,128)(2,1)} custom-call(bf16[32,2048]{1,0:T(8,128)(2,1)} %get-tuple-element.8.h_hbm, f32[32,128]{1,0:T(8,128)} %get-tuple-element.9.table_hbm, bf16[32,2048]{1,0:T(8,128)(2,1)} %get-tuple-element.10.resid_hbm, f32[384,8]{1,0:T(8,128)} %constant.7.clone.rowpat_hbm, f32[8,192]{1,0:T(8,128)} %constant.8.clone.colpat_hbm, ...), custom_call_target="tpu_custom_call" | custom-call | tf_op jit(solution)/shard_map/moe_ring/pallas_call | solution.py:602
  77.2 1.6 %copy.26 = bf16[32,2048]{1,0:T(8,128)(2,1)} copy(bf16[32,2048]{1,0:T(8,128)(2,1)} %moe_ring.1) | data formatting | bytes 262144

commit v6 on v5

--- a/solution.py
+++ b/solution.py
@@ -62,15 +62,13 @@
     rope_copy = pltpu.make_async_copy(rope_ref, rope, sem_c.at[1])
     small = [pltpu.make_async_copy(src, dst, sem_i.at[i]) for i, (src, dst) in enumerate((
         (x_hbm, x_ref), (ag_hbm, ag_ref), (pos_hbm, pos_ref), (freq_hbm, freq_ref), (fg_hbm, fg_ref), (ids_hbm, ids_ref)))]
-    for copy in small[:4]:
+    for copy in small:
         copy.start()
     kv_copy.start()
     q_copy(0).start()
     uk_copy.start()
     q_copy(1).start()
-    for copy in small[4:]:
-        copy.start()
-    for copy in small:
+    for copy in small[:4]:
         copy.wait()
 
     x = x_ref[...].astype(F32)
@@ -174,6 +172,8 @@
             cols = slice(i * dim // 2 + start, i * dim // 2 + start + width)
             res_ref[:, cols] = (x[:, cols] + dot32(o_heads[...], wo[i, :, start:start + width])).astype(BF16)
     wr_copy.wait()
+    for copy in small[4:]:
+        copy.wait()
     h = (unit_norm(res_ref[...].astype(F32)) * fg_ref[...].astype(F32).reshape(1, dim)).astype(BF16)
     h_ref[...] = h
 

time: 79 us -> 78.3 us (level)
  no operation moved by 1% of the time
where the time goes in v6:
time: 78.3 us; the launch traced here: 78.1 us
  Pallas kernels  75.9 us (97%)
  local copies, waits for them, and re-layouts  1.57 us (2%)
    pallas_call x1, Pallas kernels, moe_call(): pl.pallas_call(functools.partial(moe_kernel, n_ep, n_exp), out_shape=jax....  62.6 us
    pallas_call x1, Pallas kernels, attn_call(): pl.pallas_call(attn_kernel, out_shape=[jax.ShapeDtypeStruct((tok, dim), B...  13.3 us
    unnamed x1, local copies, waits for them, and re-layouts  1.57 us

profile of v6, /device:TPU:21, one launch (start us, length us, event | category | flops | bytes accessed | tf_op | source)
XLA Modules:
  0.0 78.1 jit_solution(9881899572564606408)
XLA Ops:
  0.6 13.3 %latent_attention.1 = (bf16[32,2048]{1,0:T(8,128)(2,1)}, bf16[32,2048]{1,0:T(8,128)(2,1)}, f32[32,128]{1,0:T(8,128)}, bf16[32,64,512]{2,1,0:T(8,128)(2,1)}, bf16[32,64,64]{2,1,0:T(8,128)(2,1)}) custom-call(s32[32]{0:T(128)} %pos_hbm.1, bf16[32,2048]{1,0:T(8,128)(2,1)} %x_hbm.1, f32[1,32]{1,0:T(1,128)} %constant.6.clone.freq_hbm, s32[6,32]{1,0:T(8,128)} %bitcast.5, ...), custom_call_target="tpu_custom_call" | custom-call | tf_op jit(solution)/shard_map/latent_attention/pallas_call | solution.py:207
  13.9 62.6 %moe_ring.1 = bf16[32,2048]{1,0:T(8,128)(2,1)} custom-call(bf16[32,2048]{1,0:T(8,128)(2,1)} %get-tuple-element.8.h_hbm, f32[32,128]{1,0:T(8,128)} %get-tuple-element.9.table_hbm, bf16[32,2048]{1,0:T(8,128)(2,1)} %get-tuple-element.10.resid_hbm, f32[384,8]{1,0:T(8,128)} %constant.7.clone.rowpat_hbm, f32[8,192]{1,0:T(8,128)} %constant.8.clone.colpat_hbm, ...), custom_call_target="tpu_custom_call" | custom-call | tf_op jit(solution)/shard_map/moe_ring/pallas_call | solution.py:602
  76.5 1.6 %copy.26 = bf16[32,2048]{1,0:T(8,128)(2,1)} copy(bf16[32,2048]{1,0:T(8,128)(2,1)} %moe_ring.1) | data formatting | bytes 262144
